TPU v7x, 128 devices: a whole 4x4x4 slice. The times are simulated.
128 devices in a mesh: data: 128 (over z, y, x, core).
Axes of the slice: x: 4, y: 4, z: 4, core: 2. Of those that a mesh axis runs over, the one named last changes fastest.
Arguments:
- x_now: bfloat16 [1024, 784, 128], P('data')
- labels_now: int32 [1024], P('data')
- x_next: bfloat16 [1024, 784, 128], P('data')
- up_one: float32 [2, 128, 512], replicated
- down_one: float32 [2, 512, 128], replicated
- merge_proj: float32 [512, 512], replicated
- up_two: float32 [2, 512, 2048], replicated
- down_two: float32 [2, 2048, 512], replicated
- head_proj: float32 [512, 1000], replicated
- vel_up_one: float32 [2, 128, 512], replicated
- vel_down_one: float32 [2, 512, 128], replicated
- vel_merge_proj: float32 [512, 512], replicated
- vel_up_two: float32 [2, 512, 2048], replicated
- vel_down_two: float32 [2, 2048, 512], replicated
- vel_head_proj: float32 [512, 1000], replicated
Outputs:
- output 1: float32 [1024, 1000], P('data')
- output 2: float32 [2, 128, 512], replicated
- output 3: float32 [2, 512, 128], replicated
- output 4: float32 [512, 512], replicated
- output 5: float32 [2, 512, 2048], replicated
- output 6: float32 [2, 2048, 512], replicated
- output 7: float32 [512, 1000], replicated
- output 8: float32 [2, 128, 512], replicated
- output 9: float32 [2, 512, 128], replicated
- output 10: float32 [512, 512], replicated
- output 11: float32 [2, 512, 2048], replicated
- output 12: float32 [2, 2048, 512], replicated
- output 13: float32 [512, 1000], replicated
All inputs are finite; a program needn't handle non-finite values.
Results may differ from a plain program's by a relative error of at most 0.0146127.
Values are sent between devices in bfloat16 or wider.
A program may use at most 1 GiB of HBM per device.

v0:
```python
import jax
import jax.numpy as jnp
from jax import lax
from jax.sharding import PartitionSpec as P

MOMENTUM = 0.9
TRUST = 0.1
LN_EPS = 1e-6


def layer_norm(values):
    row_mean = jnp.mean(values, axis=-1, keepdims=True)
    centered = values - row_mean
    variance = jnp.mean(centered * centered, axis=-1, keepdims=True)
    return centered * lax.rsqrt(variance + LN_EPS)


def gelu_tanh(values):
    return jax.nn.gelu(values, approximate=True)


def contract_rows(lhs_mat, rhs_mat):
    return lax.dot_general(lhs_mat, rhs_mat, (((0,), (0,)), ((), ())), preferred_element_type=jnp.float32)


def contract_cols(lhs_mat, rhs_mat):
    return lax.dot_general(lhs_mat, rhs_mat, (((1,), (1,)), ((), ())), preferred_element_type=jnp.float32)


def to_bf16_layers(stacked):
    return [stacked[layer_num].astype(jnp.bfloat16) for layer_num in range(stacked.shape[0])]


def cast_weights(params):
    up_one, down_one, merge_proj, up_two, down_two, head_proj = params
    return (to_bf16_layers(up_one), to_bf16_layers(down_one), merge_proj.astype(jnp.bfloat16), to_bf16_layers(up_two), to_bf16_layers(down_two), head_proj.astype(jnp.bfloat16))


def block_forward(residual, w_up, w_down):
    normed, norm_back = jax.vjp(layer_norm, residual.astype(jnp.float32))
    normed_b = normed.astype(jnp.bfloat16)
    pre_act = jnp.dot(normed_b, w_up, preferred_element_type=jnp.float32)
    activated, gelu_back = jax.vjp(gelu_tanh, pre_act)
    activated_b = activated.astype(jnp.bfloat16)
    block_out = jnp.dot(activated_b, w_down, preferred_element_type=jnp.float32)
    new_residual = (residual.astype(jnp.float32) + block_out).astype(jnp.bfloat16)
    return new_residual, (normed_b, activated_b, norm_back, gelu_back)


def block_backward(grad_out, saved, w_up, w_down):
    normed_b, activated_b, norm_back, gelu_back = saved
    grad_down = contract_rows(activated_b, grad_out)
    grad_act = contract_cols(grad_out, w_down)
    grad_pre = gelu_back(grad_act)[0].astype(jnp.bfloat16)
    grad_up = contract_rows(normed_b, grad_pre)
    grad_normed = contract_cols(grad_pre, w_up)
    grad_in = norm_back(grad_normed)[0] + grad_out.astype(jnp.float32)
    return grad_in.astype(jnp.bfloat16), grad_up, grad_down


def model_forward(images, weights):
    ups_one, downs_one, merge_w, ups_two, downs_two, head_w = weights
    img_count, tokens, width = images.shape
    residual = images.reshape(img_count * tokens, width)
    saved_one = []
    for w_up, w_down in zip(ups_one, downs_one):
        residual, saved = block_forward(residual, w_up, w_down)
        saved_one.append(saved)
    merged = residual.reshape(img_count * tokens // 4, 4 * width)
    residual = jnp.dot(merged, merge_w, preferred_element_type=jnp.float32).astype(jnp.bfloat16)
    saved_two = []
    for w_up, w_down in zip(ups_two, downs_two):
        residual, saved = block_forward(residual, w_up, w_down)
        saved_two.append(saved)
    pooled = jnp.mean(residual.reshape(img_count, tokens // 4, -1), axis=1, dtype=jnp.float32)
    head_in, head_back = jax.vjp(layer_norm, pooled)
    head_in_b = head_in.astype(jnp.bfloat16)
    logits = jnp.dot(head_in_b, head_w, preferred_element_type=jnp.float32)
    return logits, (saved_one, merged, saved_two, head_in_b, head_back)


def loss_grad(logits, labels, global_batch):
    soft_probs = jax.nn.softmax(logits, axis=-1)
    class_ids = jnp.arange(logits.shape[1], dtype=jnp.int32)
    onehot = (labels[:, None] == class_ids[None, :]).astype(jnp.float32)
    return ((soft_probs - onehot) / global_batch).astype(jnp.bfloat16)


def head_input_grad(grad_logits, head_w, head_back, merged_tokens):
    grad_pooled = head_back(contract_cols(grad_logits, head_w))[0] / merged_tokens
    img_count, width_two = grad_pooled.shape
    spread = jnp.broadcast_to(grad_pooled.astype(jnp.bfloat16)[:, None, :], (img_count, merged_tokens, width_two))
    return spread.reshape(img_count * merged_tokens, width_two)


def lars_step(weight, velocity, grad_sum):
    grad_f = grad_sum.astype(jnp.float32)
    red_axes = (weight.ndim - 2, weight.ndim - 1)
    w_norm = jnp.sqrt(jnp.sum(weight * weight, axis=red_axes, keepdims=True))
    g_norm = jnp.sqrt(jnp.sum(grad_f * grad_f, axis=red_axes, keepdims=True))
    new_vel = MOMENTUM * velocity + TRUST * (w_norm / g_norm) * grad_f
    return weight - new_vel, new_vel


def finish_step(params, velocities, grad_sums, x_next):
    updated = [lars_step(weight, velocity, grad_sum) for weight, velocity, grad_sum in zip(params, velocities, grad_sums)]
    new_params = tuple(pair_new[0] for pair_new in updated)
    new_vels = tuple(pair_new[1] for pair_new in updated)
    logits_next = model_forward(x_next, cast_weights(new_params))[0]
    return (logits_next,) + new_params + new_vels


def solution(mesh):
    data_devs = mesh.shape['data']

    def local_step(x_now, labels_now, x_next, up_one, down_one, merge_proj, up_two, down_two, head_proj, vel_up_one, vel_down_one, vel_merge_proj, vel_up_two, vel_down_two, vel_head_proj):
        params = (up_one, down_one, merge_proj, up_two, down_two, head_proj)
        velocities = (vel_up_one, vel_down_one, vel_merge_proj, vel_up_two, vel_down_two, vel_head_proj)
        weights = cast_weights(params)
        ups_one, downs_one, merge_w, ups_two, downs_two, head_w = weights
        img_count, tokens, width = x_now.shape
        depth_one = len(ups_one)
        depth_two = len(ups_two)
        logits, saved = model_forward(x_now, weights)
        saved_one, merged, saved_two, head_in_b, head_back = saved
        grad_logits = loss_grad(logits, labels_now, img_count * data_devs)
        sum_head = lax.psum(contract_rows(head_in_b, grad_logits).astype(jnp.bfloat16), 'data')
        grad_resid = head_input_grad(grad_logits, head_w, head_back, tokens // 4)
        sums_up_two = [None] * depth_two
        sums_down_two = [None] * depth_two
        for layer_num in reversed(range(depth_two)):
            grad_resid, grad_up, grad_down = block_backward(grad_resid, saved_two[layer_num], ups_two[layer_num], downs_two[layer_num])
            sums_down_two[layer_num] = lax.psum(grad_down.astype(jnp.bfloat16), 'data')
            sums_up_two[layer_num] = lax.psum(grad_up.astype(jnp.bfloat16), 'data')
        sum_merge = lax.psum(contract_rows(merged, grad_resid).astype(jnp.bfloat16), 'data')
        grad_resid = contract_cols(grad_resid, merge_w).astype(jnp.bfloat16).reshape(img_count * tokens, width)
        sums_up_one = [None] * depth_one
        sums_down_one = [None] * depth_one
        for layer_num in reversed(range(depth_one)):
            grad_resid, grad_up, grad_down = block_backward(grad_resid, saved_one[layer_num], ups_one[layer_num], downs_one[layer_num])
            sums_down_one[layer_num] = lax.psum(grad_down.astype(jnp.bfloat16), 'data')
            sums_up_one[layer_num] = lax.psum(grad_up.astype(jnp.bfloat16), 'data')
        grad_sums = (jnp.stack(sums_up_one), jnp.stack(sums_down_one), sum_merge, jnp.stack(sums_up_two), jnp.stack(sums_down_two), sum_head)
        return finish_step(params, velocities, grad_sums, x_next)

    replicated = P()
    batch_split = P('data')
    in_specs = (batch_split, batch_split, batch_split) + (replicated,) * 12
    out_specs = (batch_split,) + (replicated,) * 12
    return jax.shard_map(local_step, mesh=mesh, in_specs=in_specs, out_specs=out_specs, check_vma=False)
```

profile of v0, /device:TPU:1, one launch (start us, length us, event | category | flops | bytes accessed | tf_op | source)
XLA Modules:
  0.0 514.1 jit_solution(11922756083430637253)
XLA Ops:
  19.6 10.0 %multiply_reduce_fusion.1 = (f32[2]{0:T(128)}, bf16[2,512,2048]{2,1,0:T(8,128)(2,1)}) fusion(f32[2,512,2048]{2,1,0:T(8,128)} %param.21), kind=kLoop, calls=%fused_computation.95 | loop fusion | flops 6291454 | bytes 12582920 | tf_op jit(solution)/shard_map/reduce_sum | solution.py:99
  31.7 4.6 fusion.214
  36.8 7.9 %multiply_convert_fusion.2 = (bf16[6272,512]{1,0:T(8,128)(2,1)S(1)}, f32[6272,512]{1,0:T(8,128)}) fusion(bf16[2,128,512]{2,1,0:T(8,128)(2,1)S(1)} %get-tuple-element.44, f32[6272,128]{0,1:T(8,128)S(1)} %get-tuple-element.46, f32[6272]{0:T(1024)S(1)} %fusion.165, f32[6272]{0:T(1024)S(1)} %broadcast_multiply_fusion.1), kind=kOutput, calls=%fused_computation.74 | convolution fusion | flops 853393408 | bytes 22667264 | tf_op jit(solution)/shard_map/dot_general | solution.py:42
  56.8 6.9 %fusion.108 = f32[1568,2048]{1,0:T(8,128)} fusion(bf16[2,512,2048]{2,1,0:T(8,128)(2,1)S(1)} %copy-done.22, bf16[1568,512]{1,0:T(8,128)(2,1)S(1)} %get-tuple-element.50, f32[1568]{0:T(1024)S(1)} %fusion.169, f32[1568]{0:T(1024)S(1)} %broadcast_multiply_fusion.7), kind=kOutput, calls=%fused_computation.184 | convolution fusion | flops 3291545600 | bytes 16564224 | tf_op jit(solution)/shard_map/dot_general | solution.py:42
  63.7 8.5 %convert_reduce_fusion.2 = (f32[1568]{0:T(1024)S(1)}, bf16[1568,512]{1,0:T(8,128)(2,1)S(1)}) fusion(f32[2,2048,512]{2,1,0:T(8,128)S(1)} %bitcast.128, f32[1568,2048]{1,0:T(8,128)} %fusion.108, bf16[1568,512]{1,0:T(8,128)(2,1)S(1)} %get-tuple-element.50), kind=kOutput, calls=%fused_computation.107 | convolution fusion | flops 3321248256 | bytes 18159744 | tf_op jit(solution)/shard_map/dot_general | solution.py:45
  73.1 7.1 %fusion.110 = f32[1568,2048]{1,0:T(8,128)} fusion(bf16[2,512,2048]{2,1,0:T(8,128)(2,1)S(1)} %copy-done.22, bf16[1568,512]{1,0:T(8,128)(2,1)S(1)} %get-tuple-element.52, f32[1568]{0:T(1024)S(1)} %fusion.170, f32[1568]{0:T(1024)S(1)} %broadcast_multiply_fusion.6), kind=kOutput, calls=%fused_computation.186 | convolution fusion | flops 3291545600 | bytes 16564224 | tf_op jit(solution)/shard_map/dot_general | solution.py:42
  80.1 7.8 %fusion.97 = f32[1568,512]{1,0:T(8,128)S(1)} fusion(bf16[1568,512]{1,0:T(8,128)(2,1)S(1)} %get-tuple-element.52, f32[2,2048,512]{2,1,0:T(8,128)S(1)} %bitcast.128, f32[1568,2048]{1,0:T(8,128)} %fusion.110), kind=kOutput, calls=%fused_computation.158 | convolution fusion | flops 3320446976 | bytes 19759104 | tf_op jit(solution)/shard_map/dot_general | solution.py:45
  96.0 9.2 %fusion.101 = bf16[1,2048,512]{2,1,0:T(8,128)(2,1)} fusion(bf16[1568,512]{1,0:T(8,128)(2,1)S(1)} %reshape.354, f32[1568,2048]{1,0:T(8,128)} %fusion.110), kind=kOutput, calls=%fused_computation.166 | convolution fusion | flops 3318284288 | bytes 16547840 | tf_op jit(solution)/shard_map/dot_general | solution.py:23
  105.2 15.0 %fusion.27 = bf16[1568,2048]{1,0:T(8,128)(2,1)} fusion(f32[1568,2048]{1,0:T(8,128)} %fusion.110, bf16[1568,512]{1,0:T(8,128)(2,1)S(1)} %reshape.354, f32[2,2048,512]{2,1,0:T(8,128)} %param.22), kind=kOutput, calls=%fused_computation.39 | convolution fusion | flops 3352559616 | bytes 22970368 | tf_op jit(solution)/shard_map/dot_general | solution.py:27
  120.2 8.8 %fusion.99 = bf16[1,512,2048]{2,1,0:T(8,128)(2,1)} fusion(bf16[1568,2048]{1,0:T(8,128)(2,1)} %fusion.27, bf16[1568,512]{1,0:T(8,128)(2,1)S(1)} %copy-done.12, f32[1568]{0:T(1024)S(1)} %fusion.170, f32[1568]{0:T(1024)S(1)} %broadcast_multiply_fusion.6), kind=kOutput, calls=%fused_computation.164 | convolution fusion | flops 3292594176 | bytes 10137856 | tf_op jit(solution)/shard_map/dot_general | solution.py:23
  129.0 3.9 fusion.92
  135.8 9.4 %fusion.100 = bf16[1,2048,512]{2,1,0:T(8,128)(2,1)} fusion(bf16[1568,512]{1,0:T(8,128)(2,1)S(1)} %add_convert_fusion.2, f32[1568,2048]{1,0:T(8,128)} %fusion.108), kind=kOutput, calls=%fused_computation.165 | convolution fusion | flops 3318284288 | bytes 16547840 | tf_op jit(solution)/shard_map/dot_general | solution.py:23
  145.2 13.4 %fusion.20 = bf16[1568,2048]{1,0:T(8,128)(2,1)S(1)} fusion(f32[1568,2048]{1,0:T(8,128)} %fusion.108, bf16[1568,512]{1,0:T(8,128)(2,1)S(1)} %add_convert_fusion.2, f32[2,2048,512]{2,1,0:T(8,128)S(1)} %bitcast.130), kind=kOutput, calls=%fused_computation.32 | convolution fusion | flops 3352559616 | bytes 22970368 | tf_op jit(solution)/shard_map/dot_general | solution.py:27
  158.6 4.0 fusion.88
  162.5 5.6 %fusion.98 = bf16[1,512,2048]{2,1,0:T(8,128)(2,1)} fusion(bf16[1568,2048]{1,0:T(8,128)(2,1)S(1)} %fusion.20, bf16[1568,512]{1,0:T(8,128)(2,1)S(1)} %copy-done.10, f32[1568]{0:T(1024)S(1)} %copy-done.51, f32[1568]{0:T(1024)S(1)} %copy-done.47), kind=kOutput, calls=%fused_computation.163 | convolution fusion | flops 3292594176 | bytes 10137856 | tf_op jit(solution)/shard_map/dot_general | solution.py:23
  175.0 5.4 %fusion.132 = bf16[1,512,128]{2,1,0:T(8,128)(2,1)} fusion(bf16[6272,512]{1,0:T(8,128)(2,1)} %copy-done.7, bf16[6272,128]{1,0:T(8,128)(2,1)S(1)} %reshape.355), kind=kOutput, calls=%fused_computation.205 | convolution fusion | flops 822149120 | bytes 8159232 | tf_op jit(solution)/shard_map/dot_general | solution.py:23
  182.1 11.7 %fusion.13 = bf16[6272,512]{1,0:T(8,128)(2,1)S(1)} fusion(f32[6272,512]{1,0:T(8,128)} %get-tuple-element.48, bf16[6272,128]{1,0:T(8,128)(2,1)S(1)} %reshape.355, f32[2,512,128]{2,1,0:T(8,128)} %param.19), kind=kOutput, calls=%fused_computation.25 | convolution fusion | flops 886308864 | bytes 21004288 | tf_op jit(solution)/shard_map/dot_general | solution.py:27
  202.1 5.7 %fusion.131 = bf16[1,512,128]{2,1,0:T(8,128)(2,1)} fusion(bf16[6272,128]{0,1:T(8,128)(2,1)S(1)} %add_convert_fusion, f32[6272,512]{1,0:T(8,128)S(1)} %bitcast.135), kind=kOutput, calls=%fused_computation.204 | convolution fusion | flops 851050496 | bytes 14581760 | tf_op jit(solution)/shard_map/dot_general | solution.py:23
  207.8 15.7 %fusion.133 = bf16[1,128,512]{2,1,0:T(8,128)(2,1)} fusion(f32[6272,512]{1,0:T(8,128)} %copy-done.8, bf16[6272,128]{0,1:T(8,128)(2,1)} %copy-done.30, f32[6272]{0:T(1024)S(1)} %copy-done.53, f32[6272]{0:T(1024)S(1)} %copy-done.52, f32[2,512,128]{2,1,0:T(8,128)S(1)} %copy-done.26, bf16[6272,128]{1,0:T(8,128)(2,1)S(1)} %bitcast.132), kind=kOutput, calls=%fused_computation.206 | convolution fusion | flops 1711669248 | bytes 16375808 | tf_op jit(solution)/shard_map/dot_general | solution.py:23
  228.5 3.9 copy.36
  240.8 4.6 multiply_reduce_fusion
  245.4 149.9 %all-reduce.3.cloned.1.call-done = (bf16[512,1000]{0,1:T(8,128)(2,1)}, bf16[1,512,128]{2,1,0:T(8,128)(2,1)}, bf16[1,512,128]{2,1,0:T(8,128)(2,1)}, bf16[1,128,51...) async-done(((bf16[512,1000]{0,1:T(8,128)(2,1)}, ...) | async-done | bytes 10461200 | tf_op jit(solution)/shard_map/psum | solution.py:127
  407.3 8.2 %fusion.216 = (f32[6272]{0:T(1024)S(1)}, f32[6272,128]{0,1:T(8,128)}) fusion(f32[6272,128]{0,1:T(8,128)} %copy.36, bf16[2,512,128]{2,1,0:T(8,128)(2,1)} %get-tuple-element.34, bf16[6272,128]{1,0:T(8,128)(2,1)} %bitcast.137, bf16[2,128,512]{2,1,0:T(8,128)(2,1)} %get-tuple-element.31), kind=kOutput, calls=%fused_computation.332 | convolution fusion | flops 1676273536 | bytes 8315392 | tf_op jit(solution)/shard_map/dot_general | solution.py:45
  417.8 8.6 %fusion.65 = bf16[6272,128]{0,1:T(8,128)(2,1)} fusion(f32[6272,128]{0,1:T(8,128)} %get-tuple-element.64, f32[6272]{0:T(1024)S(1)} %add_rsqrt_fusion, f32[6272]{0:T(1024)S(1)} %broadcast_multiply_fusion, bf16[2,512,128]{2,1,0:T(8,128)(2,1)} %get-tuple-element.34, bf16[2,128,512]{2,1,0:T(8,128)(2,1)S(1)} %copy-done.43), kind=kOutput, calls=%fused_computation.89 | convolution fusion | flops 1677082624 | bytes 8347648 | tf_op jit(solution)/shard_map/dot_general | solution.py:45
  426.5 3.7 copy.38
  430.2 3.7 reshape.356
  444.3 11.6 %fusion.201 = (bf16[2,512,2048]{2,1,0:T(8,128)(2,1)}, f32[2,512,2048]{2,1,0:T(8,128)}, f32[2,512,2048]{2,1,0:T(8,128)}) fusion(f32[2,512,2048]{2,1,0:T(8,128)S(1)} %bitcast.126, bf16[1,512,2048]{2,1,0:T(8,128)(2,1)} %get-tuple-element.21, bf16[1,512,2048]{2,1,0:T(8,128)(2,1)} %get-tuple-element.22, f32[2]{0:T(128)S(1)} %multiply_multiply_fusion.16, ...), kind=kLoop, calls=%fused_computation.323 | loop fusion | flops 14680064 | bytes 41943048 | tf_op jit(solution)/shard_map/convert.7
  455.9 13.1 %fusion.203 = (bf16[2,2048,512]{2,1,0:T(8,128)(2,1)}, f32[2,2048,512]{2,1,0:T(8,128)}, f32[2,2048,512]{2,1,0:T(8,128)}) fusion(f32[2,2048,512]{2,1,0:T(8,128)} %param.22, bf16[1,2048,512]{2,1,0:T(8,128)(2,1)S(1)} %copy-done.13, bf16[1,2048,512]{2,1,0:T(8,128)(2,1)} %get-tuple-element.20, f32[2]{0:T(128)S(1)} %multiply_multiply_fusion.15, ...), kind=kLoop, calls=%fused_computation.324 | loop fusion | flops 14680064 | bytes 41943048 | tf_op jit(solution)/shard_map/convert.6
  469.0 12.2 %convert_reduce_fusion = (f32[1568]{0:T(1024)S(1)}, bf16[1568,512]{1,0:T(8,128)(2,1)}) fusion(bf16[2,2048,512]{2,1,0:T(8,128)(2,1)} %get-tuple-element.26, bf16[2,512,2048]{2,1,0:T(8,128)(2,1)} %get-tuple-element.23, bf16[1568,512]{1,0:T(8,128)(2,1)} %copy-done.31, f32[1568]{0:T(1024)S(1)} %add_rsqrt_fusion.4, f32[1568]{0:T(1024)S(1)} %broadcast_multiply_fusion.5), kind=kOutput, calls=%fused_computation.98 | convolution fusion | flops 6612793856 | bytes 9030016 | tf_op jit(solution)/shard_map/dot_general | solution.py:45
  483.3 12.8 %fusion.96 = f32[1568,512]{1,0:T(8,128)} fusion(bf16[1568,512]{1,0:T(8,128)(2,1)} %get-tuple-element.68, bf16[2,2048,512]{2,1,0:T(8,128)(2,1)} %get-tuple-element.26, bf16[2,512,2048]{2,1,0:T(8,128)(2,1)} %get-tuple-element.23, f32[1568]{0:T(1024)S(1)} %add_rsqrt_fusion.3, f32[1568]{0:T(1024)S(1)} %broadcast_multiply_fusion.4), kind=kOutput, calls=%fused_computation.157 | convolution fusion | flops 6611992576 | bytes 10629376 | tf_op jit(solution)/shard_map/dot_general | solution.py:45
  496.1 3.3 reshape.360
  502.1 3.6 fusion.211
  (236 shorter events, 96.6 us)
Async XLA Ops:
  7.2 6.7 %copy-start.4 = (bf16[8,784,128]{2,1,0:T(8,128)(2,1)S(1)}, bf16[8,784,128]{2,1,0:T(8,128)(2,1)}, u32[]{:S(2)}) copy-start(bf16[8,784,128]{2,1,0:T(8,128)(2,1)} %param.15) | copy-start | bytes 4816900
  7.2 388.1 %all-reduce.3.cloned.1.call-start = ((), (), s32[]{:S(2)}) async-start(), calls=%async_computation | async-start | bytes 20922368 | tf_op jit(solution)/shard_map/psum | solution.py:127
  16.8 20.1 %copy-start.35 = (bf16[2,128,512]{2,1,0:T(8,128)(2,1)}, bf16[2,128,512]{2,1,0:T(8,128)(2,1)S(1)}, u32[]{:S(2)}) copy-start(bf16[2,128,512]{2,1,0:T(8,128)(2,1)S(1)} %get-tuple-element.44) | copy-start | bytes 786436
  36.4 8.4 %copy-start = (f32[6272,128]{0,1:T(8,128)}, f32[6272,128]{0,1:T(8,128)S(1)}, u32[]{:S(2)}) copy-start(f32[6272,128]{0,1:T(8,128)S(1)} %get-tuple-element.46) | copy-start | bytes 9633796
  36.4 8.4 %copy-start.33 = (f32[6272]{0:T(1024)}, f32[6272]{0:T(1024)S(1)}, u32[]{:S(2)}) copy-start(f32[6272]{0:T(1024)S(1)} %broadcast_multiply_fusion.1) | copy-start | bytes 75268
  36.8 8.0 %copy-start.44 = (f32[6272]{0:T(1024)}, f32[6272]{0:T(1024)S(1)}, u32[]{:S(2)}) copy-start(f32[6272]{0:T(1024)S(1)} %multiply_reduce_fusion.4) | copy-start | bytes 75268
  36.8 8.0 %copy-start.41 = (f32[6272]{0:T(1024)}, f32[6272]{0:T(1024)S(1)}, u32[]{:S(2)}) copy-start(f32[6272]{0:T(1024)S(1)} %fusion.165) | copy-start | bytes 75268
  52.3 11.4 %slice-start.2 = ((s8[8388608]{0:T(1024)(128)(4,1)}), s8[4194304]{0:T(1024)(128)(4,1)S(1)}, s32[]{:S(2)}) async-start(s8[8388608]{0:T(1024)(128)(4,1)} %bitcast.127), calls=%async_computation.3 | async-start | bytes 8388608
  55.3 8.4 %copy-start.9 = (bf16[1568,512]{1,0:T(8,128)(2,1)}, bf16[1568,512]{1,0:T(8,128)(2,1)S(1)}, u32[]{:S(2)}) copy-start(bf16[1568,512]{1,0:T(8,128)(2,1)S(1)} %get-tuple-element.50) | copy-start | bytes 4816900
  56.8 6.9 %slice-start.3 = ((s8[8388608]{0:T(1024)(128)(4,1)}), s8[4194304]{0:T(1024)(128)(4,1)S(1)}, s32[]{:S(2)}) async-start(s8[8388608]{0:T(1024)(128)(4,1)} %bitcast.127), calls=%async_computation.4 | async-start | bytes 8388608
  72.2 7.9 %copy-start.11 = (bf16[1568,512]{1,0:T(8,128)(2,1)}, bf16[1568,512]{1,0:T(8,128)(2,1)S(1)}, u32[]{:S(2)}) copy-start(bf16[1568,512]{1,0:T(8,128)(2,1)S(1)} %get-tuple-element.52) | copy-start | bytes 4816900
  105.2 15.0 %copy-start.12 = (bf16[1568,512]{1,0:T(8,128)(2,1)S(1)}, bf16[1568,512]{1,0:T(8,128)(2,1)}, u32[]{:S(2)}) copy-start(bf16[1568,512]{1,0:T(8,128)(2,1)} %copy-done.11) | copy-start | bytes 4816900
  120.2 8.9 %copy-start.23 = (bf16[2,512,2048]{2,1,0:T(8,128)(2,1)S(1)}, bf16[2,512,2048]{2,1,0:T(8,128)(2,1)}, u32[]{:S(2)}) copy-start(bf16[2,512,2048]{2,1,0:T(8,128)(2,1)} %get-tuple-element.42) | copy-start | bytes 12582916
  120.2 8.9 %copy-start.57 = (bf16[1568,2048]{1,0:T(8,128)(2,1)S(1)}, bf16[1568,2048]{1,0:T(8,128)(2,1)}, u32[]{:S(2)}) copy-start(bf16[1568,2048]{1,0:T(8,128)(2,1)} %fusion.27) | copy-start | bytes 19267588
  134.2 10.9 %slice-start.4 = ((s8[8388608]{0:T(1024)(128)(4,1)}), s8[4194304]{0:T(1024)(128)(4,1)S(1)}, s32[]{:S(2)}) async-start(s8[8388608]{0:T(1024)(128)(4,1)} %bitcast.129), calls=%async_computation.5 | async-start | bytes 8388608
  135.8 9.4 %slice-start.5 = ((s8[8388608]{0:T(1024)(128)(4,1)}), s8[4194304]{0:T(1024)(128)(4,1)S(1)}, s32[]{:S(2)}) async-start(s8[8388608]{0:T(1024)(128)(4,1)} %bitcast.129), calls=%async_computation.6 | async-start | bytes 8388608
  145.2 13.4 %copy-start.10 = (bf16[1568,512]{1,0:T(8,128)(2,1)S(1)}, bf16[1568,512]{1,0:T(8,128)(2,1)}, u32[]{:S(2)}) copy-start(bf16[1568,512]{1,0:T(8,128)(2,1)} %copy-done.9) | copy-start | bytes 4816900
  145.2 13.4 %copy-start.47 = (f32[1568]{0:T(1024)S(1)}, f32[1568]{0:T(1024)}, u32[]{:S(2)}) copy-start(f32[1568]{0:T(1024)} %copy-done.46) | copy-start | bytes 18820
  162.5 5.6 %copy-start.49 = (f32[1568]{0:T(1024)S(1)}, f32[1568]{0:T(1024)}, u32[]{:S(2)}) copy-start(f32[1568]{0:T(1024)} %copy-done.48) | copy-start | bytes 18820
  182.1 11.7 %copy-start.1 = (f32[6272,128]{0,1:T(8,128)S(1)}, f32[6272,128]{0,1:T(8,128)}, u32[]{:S(2)}) copy-start(f32[6272,128]{0,1:T(8,128)} %copy-done) | copy-start | bytes 9633796
  182.1 11.7 %copy-start.34 = (f32[6272]{0:T(1024)S(1)}, f32[6272]{0:T(1024)}, u32[]{:S(2)}) copy-start(f32[6272]{0:T(1024)} %copy-done.33) | copy-start | bytes 75268
  182.1 11.7 %copy-start.42 = (f32[6272]{0:T(1024)S(1)}, f32[6272]{0:T(1024)}, u32[]{:S(2)}) copy-start(f32[6272]{0:T(1024)} %copy-done.41) | copy-start | bytes 75268
  195.5 5.3 %slice-start.7 = ((s8[12845056]{0:T(1024)(128)(4,1)}), s8[4194304]{0:T(1024)(128)(4,1)S(1)}, s32[]{:S(2)}) async-start(s8[12845056]{0:T(1024)(128)(4,1)} %bitcast.134), calls=%async_computation.8 | async-start | bytes 8388608
  202.1 5.7 %copy-start.5 = (bf16[8,784,128]{2,1,0:T(8,128)(2,1)S(1)}, bf16[8,784,128]{2,1,0:T(8,128)(2,1)}, u32[]{:S(2)}) copy-start(bf16[8,784,128]{2,1,0:T(8,128)(2,1)} %param.15) | copy-start | bytes 4816900
  202.1 5.7 %copy-start.26 = (f32[2,512,128]{2,1,0:T(8,128)S(1)}, f32[2,512,128]{2,1,0:T(8,128)}, u32[]{:S(2)}) copy-start(f32[2,512,128]{2,1,0:T(8,128)} %param.19) | copy-start | bytes 1572868
  202.1 5.7 %copy-start.52 = (f32[6272]{0:T(1024)S(1)}, f32[6272]{0:T(1024)}, u32[]{:S(2)}) copy-start(f32[6272]{0:T(1024)} %div.154) | copy-start | bytes 75268
  202.1 5.7 %copy-start.53 = (f32[6272]{0:T(1024)S(1)}, f32[6272]{0:T(1024)}, u32[]{:S(2)}) copy-start(f32[6272]{0:T(1024)} %rsqrt.122) | copy-start | bytes 75268
  240.8 162.6 %copy-start.56 = (f32[2]{0:T(128)S(1)}, f32[2]{0:T(128)}, u32[]{:S(2)}) copy-start(f32[2]{0:T(128)} %get-tuple-element.43) | copy-start | bytes 28
  395.3 10.7 %copy-start.38 = (bf16[1,512,128]{2,1,0:T(8,128)(2,1)S(1)}, bf16[1,512,128]{2,1,0:T(8,128)(2,1)}, u32[]{:S(2)}) copy-start(bf16[1,512,128]{2,1,0:T(8,128)(2,1)} %get-tuple-element.14) | copy-start | bytes 393220
  395.3 10.7 %copy-start.39 = (bf16[1,512,128]{2,1,0:T(8,128)(2,1)S(1)}, bf16[1,512,128]{2,1,0:T(8,128)(2,1)}, u32[]{:S(2)}) copy-start(bf16[1,512,128]{2,1,0:T(8,128)(2,1)} %get-tuple-element.15) | copy-start | bytes 393220
  437.6 5.8 %slice-start = ((s8[8388608]{0:T(1024)(128)(4,1)}), s8[4194304]{0:T(1024)(128)(4,1)S(1)}, s32[]{:S(2)}) async-start(s8[8388608]{0:T(1024)(128)(4,1)} %bitcast.125), calls=%async_computation.1 | async-start | bytes 8388608
  438.8 5.5 %slice-start.1 = ((s8[8388608]{0:T(1024)(128)(4,1)}), s8[4194304]{0:T(1024)(128)(4,1)S(1)}, s32[]{:S(2)}) async-start(s8[8388608]{0:T(1024)(128)(4,1)} %bitcast.125), calls=%async_computation.2 | async-start | bytes 8388608
  (37 other events, 101.6 us)
Sparse Core Ops, SparseCore 0:
  223.7 171.6 all-reduce.2
where the time goes:
time: 523 us; the launch traced here: 514 us
  matrix products  211 us (40%)
  waiting for transfers between devices  150 us (29%)
  other arithmetic  98.1 us (19%)
  local copies, waits for them, and re-layouts  37.2 us (7%)
  between operations  17.9 us (3%)
    psum x1, waiting for transfers between devices, local_step(): lax.psum(contract_rows(head_in_b, grad_logits).astype(jnp.bfloat16), 'data')  150 us
    dot_general x10, matrix products, contract_rows(): lax.dot_general(lhs_mat, rhs_mat, (((0,), (0,)), ((), ())), preferred_ele...  64.9 us
    dot_general x8, matrix products, block_forward(): block_out = jnp.dot(activated_b, w_down, preferred_element_type=jnp.float32)  64.8 us
    dot_general x8, matrix products, contract_cols(): lax.dot_general(lhs_mat, rhs_mat, (((1,), (1,)), ((), ())), preferred_ele...  51.6 us
    another operation x4, other arithmetic  28.5 us
    dot_general x4, matrix products, block_forward(): pre_act = jnp.dot(normed_b, w_up, preferred_element_type=jnp.float32)  23.8 us
    reduce_sum x6, other arithmetic, lars_step(): w_norm = jnp.sqrt(jnp.sum(weight * weight, axis=red_axes, keepdims=True))  18.6 us
    reduce_sum x10, other arithmetic, layer_norm(): variance = jnp.mean(centered * centered, axis=-1, keepdims=True)  12.8 us
  transfers between devices with their start and end apart: 1, of which 1 were waited for; matrix products, arithmetic and copies ran while one was open for 4% of the time, Pallas kernels for 0%

commit v1 on v0

v1 whole, which is shorter than its diff:
```python
import functools

import jax
import jax.numpy as jnp
from jax import lax
from jax.experimental import pallas as pl
from jax.experimental.pallas import tpu as pltpu
from jax.sharding import PartitionSpec as P

MOMENTUM = 0.9
TRUST = 0.1
LN_EPS = 1e-6
GELU_A = 0.7978845608028654
GELU_B = GELU_A * 0.044715
ROWS = 1568
ROWS_PAD = 1792
PER_IMAGE = 196
W1 = 128
W2 = 512
H1 = 512
H2 = 2048
CHUNK = 256
NCH = H2 // CHUNK
TILE = 224
NT = ROWS // TILE
SPLIT = 784
VMEM_LIMIT = 63 * 1024 * 1024
F32 = jnp.float32
BF16 = jnp.bfloat16


def dot_nn(lhs, rhs):
    return lax.dot_general(lhs, rhs, (((1,), (0,)), ((), ())), preferred_element_type=F32)


def dot_nt(lhs, rhs):
    return lax.dot_general(lhs, rhs, (((1,), (1,)), ((), ())), preferred_element_type=F32)


def dot_tn(lhs, rhs):
    return lax.dot_general(lhs, rhs, (((0,), (0,)), ((), ())), preferred_element_type=F32)


def ln_parts(values):
    row_mean = jnp.mean(values, axis=-1, keepdims=True)
    centered = values - row_mean
    variance = jnp.mean(centered * centered, axis=-1, keepdims=True)
    inv = lax.rsqrt(variance + LN_EPS)
    return centered * inv, inv


def ln_back(normed, inv, grad):
    mean_grad = jnp.mean(grad, axis=-1, keepdims=True)
    mean_dot = jnp.mean(grad * normed, axis=-1, keepdims=True)
    return inv * (grad - mean_grad - normed * mean_dot)


def gelu_fwd(pre):
    sq = pre * pre
    tan = jnp.tanh(pre * (GELU_A + GELU_B * sq))
    half = 0.5 * pre
    return half + half * tan


def gelu_both(pre):
    sq = pre * pre
    tan = jnp.tanh(pre * (GELU_A + GELU_B * sq))
    half = 0.5 * pre
    act = half + half * tan
    slope = (0.5 + 0.5 * tan) + (half * (1.0 - tan * tan)) * (GELU_A + (3.0 * GELU_B) * sq)
    return act, slope


def fold_sq(mat):
    rows, cols = mat.shape
    return jnp.sum((mat * mat).reshape(rows // 8, 8, cols), axis=0)


def lars_block(weight, vel, grad, scale):
    new_vel = MOMENTUM * vel + scale * grad.astype(F32)
    return weight - new_vel, new_vel


def params(**kwargs):
    return pltpu.CompilerParams(vmem_limit_bytes=VMEM_LIMIT, **kwargs)


def whole(shape):
    zeros = (0,) * len(shape)
    return pl.BlockSpec(shape, lambda *_: zeros)


def stage_one_tile(x_tile, ub, vb, mb):
    outs0, outs1 = [], []
    for quarter in range(4):
        resid = x_tile[:, quarter * W1:(quarter + 1) * W1]
        for layer in range(2):
            normed = ln_parts(resid.astype(F32))[0].astype(BF16)
            act = gelu_fwd(dot_nn(normed, ub[layer])).astype(BF16)
            resid = (resid.astype(F32) + dot_nn(act, vb[layer])).astype(BF16)
            (outs0, outs1)[layer].append(resid)
    mid = jnp.concatenate(outs0, axis=1)
    merged = jnp.concatenate(outs1, axis=1)
    return mid, merged, dot_nn(merged, mb[...]).astype(BF16)


def stage_one_now(x, up_one, down_one, merge):
    def kernel(x_ref, u_ref, v_ref, m_ref, mid_ref, merged_ref, res_ref, ub_ref, vb_ref, mb_ref, su_ref, sv_ref, sm_ref):
        @pl.when(pl.program_id(0) == 0)
        def _():
            ub_ref[...] = u_ref[...].astype(BF16)
            vb_ref[...] = v_ref[...].astype(BF16)
            mb_ref[...] = m_ref[...].astype(BF16)
            for layer in range(2):
                su_ref[layer] = fold_sq(u_ref[layer])
                sv_ref[layer] = fold_sq(v_ref[layer])
            sm_ref[...] = fold_sq(m_ref[...])

        mid, merged, res = stage_one_tile(x_ref[...], ub_ref, vb_ref, mb_ref)
        mid_ref[...] = mid
        merged_ref[...] = merged
        res_ref[...] = res

    tile = pl.BlockSpec((TILE, W2), lambda i: (i, 0))
    act = jax.ShapeDtypeStruct((ROWS, W2), BF16)
    small = [((2, W1, H1), BF16), ((2, H1, W1), BF16), ((W2, W2), BF16), ((2, 8, H1), F32), ((2, 8, W1), F32), ((8, W2), F32)]
    return pl.pallas_call(
        kernel,
        grid=(NT,),
        in_specs=[tile, whole((2, W1, H1)), whole((2, H1, W1)), whole((W2, W2))],
        out_specs=[tile] * 3 + [whole(s) for s, _ in small],
        out_shape=[act] * 3 + [jax.ShapeDtypeStruct(s, d) for s, d in small],
        compiler_params=params(),
        name="stage_one_now",
    )(x, up_one, down_one, merge)


def stage_one_next(x, scales, weights, vels, grads):
    def kernel(sc_ref, x_ref, u_ref, v_ref, m_ref, pu_ref, pv_ref, pm_ref, gu_ref, gv_ref, gm_ref, res_ref, nu_ref, nv_ref, nm_ref, qu_ref, qv_ref, qm_ref, ub_ref, vb_ref, mb_ref):
        @pl.when(pl.program_id(0) == 0)
        def _():
            for layer in range(2):
                nu_ref[layer], qu_ref[layer] = lars_block(u_ref[layer], pu_ref[layer], gu_ref[layer], sc_ref[layer])
                nv_ref[layer], qv_ref[layer] = lars_block(v_ref[layer], pv_ref[layer], gv_ref[layer], sc_ref[2 + layer])
            nm_ref[...], qm_ref[...] = lars_block(m_ref[...], pm_ref[...], gm_ref[...], sc_ref[4])
            ub_ref[...] = nu_ref[...].astype(BF16)
            vb_ref[...] = nv_ref[...].astype(BF16)
            mb_ref[...] = nm_ref[...].astype(BF16)

        res_ref[...] = stage_one_tile(x_ref[...], ub_ref, vb_ref, mb_ref)[2]

    tile = pl.BlockSpec((TILE, W2), lambda i: (i, 0))
    shapes = [(2, W1, H1), (2, H1, W1), (W2, W2)]
    return pl.pallas_call(
        kernel,
        grid=(NT,),
        in_specs=[pl.BlockSpec(memory_space=pltpu.SMEM), tile] + [whole(s) for s in shapes] * 3,
        out_specs=[tile] + [whole(s) for s in shapes] * 2,
        out_shape=[jax.ShapeDtypeStruct((ROWS, W2), BF16)] + [jax.ShapeDtypeStruct(s, F32) for s in shapes] * 2,
        scratch_shapes=[pltpu.VMEM(s, BF16) for s in shapes],
        compiler_params=params(),
        name="stage_one_next",
    )(scales, x, *weights, *vels, *grads)


def row_parts():
    return [(start, SPLIT) for start in range(0, ROWS, SPLIT)]


def stage_two_start(chunk, src_ref, dst_norm, acc_ref):
    for start, size in row_parts():
        resid = src_ref[start:start + size].astype(F32)
        dst_norm[start:start + size] = ln_parts(resid)[0].astype(BF16)
        acc_ref[start:start + size] = resid


def stage_two_step(norm_ref, acc_ref, ub, vb):
    for start, size in row_parts():
        act = gelu_fwd(dot_nn(norm_ref[start:start + size], ub)).astype(BF16)
        acc_ref[start:start + size] += dot_nn(act, vb)


def pool_images(resid_ref, pool_ref):
    cols = lax.broadcasted_iota(jnp.int32, (16, ROWS_PAD), 1)
    base = lax.broadcasted_iota(jnp.int32, (16, ROWS_PAD), 0) * PER_IMAGE
    mask = ((cols >= base) & (cols < base + PER_IMAGE) & (cols < ROWS)).astype(F32).astype(BF16)
    pool_ref[...] = dot_nn(mask, resid_ref[...]) * (1.0 / PER_IMAGE)


def stage_two_now(res_in, up_two, down_two):
    def kernel(r_ref, u_ref, v_ref, mid_ref, ub_ref, vb_ref, su_ref, sv_ref, pool_ref, norm_s, acc_s, res_s):
        layer, chunk = pl.program_id(0), pl.program_id(1)

        @pl.when(chunk == 0)
        def _():
            @pl.when(layer == 0)
            def _():
                stage_two_start(chunk, r_ref, norm_s, acc_s)

            @pl.when(layer == 1)
            def _():
                stage_two_start(chunk, mid_ref, norm_s, acc_s)
            su_ref[...] = jnp.zeros_like(su_ref)
            sv_ref[...] = jnp.zeros_like(sv_ref)

        ub = u_ref[0].astype(BF16)
        vb = v_ref[0].astype(BF16)
        ub_ref[0] = ub
        vb_ref[0] = vb
        su_ref[0] += fold_sq(u_ref[0])
        sv_ref[0] += fold_sq(v_ref[0])
        stage_two_step(norm_s, acc_s, ub, vb)

        @pl.when((chunk == NCH - 1) & (layer == 0))
        def _():
            mid_ref[...] = acc_s[...].astype(BF16)

        @pl.when((chunk == NCH - 1) & (layer == 1))
        def _():
            res_s[:ROWS] = acc_s[...].astype(BF16)
            res_s[ROWS:] = jnp.zeros((ROWS_PAD - ROWS, W2), BF16)
            pool_images(res_s, pool_ref)

    u_spec = pl.BlockSpec((1, W2, CHUNK), lambda l, j: (l, 0, j))
    v_spec = pl.BlockSpec((1, CHUNK, W2), lambda l, j: (l, j, 0))
    return pl.pallas_call(
        kernel,
        grid=(2, NCH),
        in_specs=[whole((ROWS, W2)), u_spec, v_spec],
        out_specs=[whole((ROWS, W2)), u_spec, v_spec, pl.BlockSpec((1, 8, CHUNK), lambda l, j: (l, 0, 0)), pl.BlockSpec((1, 8, W2), lambda l, j: (l, 0, 0)), whole((16, W2))],
        out_shape=[jax.ShapeDtypeStruct((ROWS, W2), BF16), jax.ShapeDtypeStruct((2, W2, H2), BF16), jax.ShapeDtypeStruct((2, H2, W2), BF16), jax.ShapeDtypeStruct((2, 8, CHUNK), F32), jax.ShapeDtypeStruct((2, 8, W2), F32), jax.ShapeDtypeStruct((16, W2), F32)],
        scratch_shapes=[pltpu.VMEM((ROWS, W2), BF16), pltpu.VMEM((ROWS, W2), F32), pltpu.VMEM((ROWS_PAD, W2), BF16)],
        compiler_params=params(),
        name="stage_two_now",
    )(res_in, up_two, down_two)


def stage_two_next(res_in, scales, up_two, down_two, vel_up, vel_down, grad_up, grad_down):
    def kernel(sc_ref, r_ref, u_ref, v_ref, pu_ref, pv_ref, gu_ref, gv_ref, nu_ref, nv_ref, qu_ref, qv_ref, pool_ref, norm_s, acc_s, res_s):
        layer, chunk = pl.program_id(0), pl.program_id(1)

        @pl.when(chunk == 0)
        def _():
            @pl.when(layer == 0)
            def _():
                stage_two_start(chunk, r_ref, norm_s, acc_s)

            @pl.when(layer == 1)
            def _():
                stage_two_start(chunk, res_s, norm_s, acc_s)

        new_u, new_pu = lars_block(u_ref[0], pu_ref[0], gu_ref[0], sc_ref[layer])
        new_v, new_pv = lars_block(v_ref[0], pv_ref[0], gv_ref[0], sc_ref[2 + layer])
        nu_ref[0] = new_u
        qu_ref[0] = new_pu
        nv_ref[0] = new_v
        qv_ref[0] = new_pv
        stage_two_step(norm_s, acc_s, new_u.astype(BF16), new_v.astype(BF16))

        @pl.when(chunk == NCH - 1)
        def _():
            res_s[:ROWS] = acc_s[...].astype(BF16)

            @pl.when(layer == 1)
            def _():
                res_s[ROWS:] = jnp.zeros((ROWS_PAD - ROWS, W2), BF16)
                pool_images(res_s, pool_ref)

    u_spec = pl.BlockSpec((1, W2, CHUNK), lambda l, j: (l, 0, j))
    v_spec = pl.BlockSpec((1, CHUNK, W2), lambda l, j: (l, j, 0))
    return pl.pallas_call(
        kernel,
        grid=(2, NCH),
        in_specs=[pl.BlockSpec(memory_space=pltpu.SMEM), whole((ROWS, W2))] + [u_spec, v_spec] * 3,
        out_specs=[u_spec, v_spec] * 2 + [whole((16, W2))],
        out_shape=[jax.ShapeDtypeStruct((2, W2, H2), F32), jax.ShapeDtypeStruct((2, H2, W2), F32)] * 2 + [jax.ShapeDtypeStruct((16, W2), F32)],
        scratch_shapes=[pltpu.VMEM((ROWS, W2), BF16), pltpu.VMEM((ROWS, W2), F32), pltpu.VMEM((ROWS_PAD, W2), BF16)],
        compiler_params=params(),
        name="stage_two_next",
    )(scales, res_in, up_two, down_two, vel_up, vel_down, grad_up, grad_down)


def stage_two_back(grad_pool, res_in, res_mid, merged, up_b, down_b, merge_b):
    def kernel(gp_ref, r0_ref, r1_ref, m_ref, u_ref, v_ref, mw_ref, du_ref, dv_ref, dm_ref, gout_ref, g_s, gt_s, n_s, nt_s, act_s, pre_s, dn_s):
        step, chunk = pl.program_id(0), pl.program_id(1)

        @pl.when((step == 0) & (chunk == 0))
        def _():
            rows = lax.broadcasted_iota(jnp.int32, (ROWS, 128), 0)
            base = lax.broadcasted_iota(jnp.int32, (ROWS, 128), 1) * PER_IMAGE
            mask = ((rows >= base) & (rows < base + PER_IMAGE)).astype(F32).astype(BF16)
            g_s[...] = dot_nn(mask, gp_ref[...]).astype(BF16)
            zeros = jnp.zeros((W2, ROWS_PAD - 1536), BF16)
            gt_s[:, 1536:] = zeros
            nt_s[:, 1536:] = zeros
            gt_s[:, :ROWS] = g_s[...].T
            act_s[ROWS:] = jnp.zeros((ROWS_PAD - ROWS, CHUNK), BF16)
            pre_s[ROWS:] = jnp.zeros((ROWS_PAD - ROWS, CHUNK), BF16)

        def begin(src_ref):
            n_s[...] = ln_parts(src_ref[...].astype(F32))[0].astype(BF16)
            nt_s[:, :ROWS] = n_s[...].T
            dn_s[...] = jnp.zeros_like(dn_s)

        @pl.when((step == 0) & (chunk == 0))
        def _():
            begin(r1_ref)

        @pl.when((step == 1) & (chunk == 0))
        def _():
            begin(r0_ref)

        ub = u_ref[0]
        vb = v_ref[0]
        for start, size in row_parts():
            act, slope = gelu_both(dot_nn(n_s[start:start + size], ub))
            grad_pre = (dot_nt(g_s[start:start + size], vb) * slope).astype(BF16)
            act_s[start:start + size] = act.astype(BF16)
            pre_s[start:start + size] = grad_pre
            dn_s[start:start + size] += dot_nt(grad_pre, ub)
        du_ref[0] = dot_nn(nt_s[...], pre_s[...]).astype(BF16)
        dv_ref[0] = dot_nn(gt_s[...], act_s[...]).T.astype(BF16)

        def finish(src_ref):
            normed, inv = ln_parts(src_ref[...].astype(F32))
            g_s[...] = (ln_back(normed, inv, dn_s[...]) + g_s[...].astype(F32)).astype(BF16)

        @pl.when((step == 0) & (chunk == NCH - 1))
        def _():
            finish(r1_ref)
            gt_s[:, :ROWS] = g_s[...].T

        @pl.when((step == 1) & (chunk == NCH - 1))
        def _():
            finish(r0_ref)
            gout_ref[...] = dot_nt(g_s[...], mw_ref[...]).astype(BF16)
            dm_ref[...] = dot_tn(m_ref[...], g_s[...]).astype(BF16)

    u_spec = pl.BlockSpec((1, W2, CHUNK), lambda l, j: (1 - l, 0, j))
    v_spec = pl.BlockSpec((1, CHUNK, W2), lambda l, j: (1 - l, j, 0))
    act = whole((ROWS, W2))
    return pl.pallas_call(
        kernel,
        grid=(2, NCH),
        in_specs=[whole((128, W2)), act, act, act, u_spec, v_spec, whole((W2, W2))],
        out_specs=[u_spec, v_spec, whole((W2, W2)), act],
        out_shape=[jax.ShapeDtypeStruct((2, W2, H2), BF16), jax.ShapeDtypeStruct((2, H2, W2), BF16), jax.ShapeDtypeStruct((W2, W2), BF16), jax.ShapeDtypeStruct((ROWS, W2), BF16)],
        scratch_shapes=[pltpu.VMEM((ROWS, W2), BF16), pltpu.VMEM((W2, ROWS_PAD), BF16), pltpu.VMEM((ROWS, W2), BF16), pltpu.VMEM((W2, ROWS_PAD), BF16), pltpu.VMEM((ROWS_PAD, CHUNK), BF16), pltpu.VMEM((ROWS_PAD, CHUNK), BF16), pltpu.VMEM((ROWS, W2), F32)],
        compiler_params=params(),
        name="stage_two_back",
    )(grad_pool, res_in, res_mid, merged, up_b, down_b, merge_b)


def stage_one_back(grad_in, x, mid, up_b, down_b):
    def kernel(g_ref, x_ref, mid_ref, u_ref, v_ref, du_ref, dv_ref, du_s, dv_s):
        tile_id = pl.program_id(0)

        @pl.when(tile_id == 0)
        def _():
            du_s[...] = jnp.zeros_like(du_s)
            dv_s[...] = jnp.zeros_like(dv_s)

        for quarter in range(4):
            cols = slice(quarter * W1, (quarter + 1) * W1)
            grad = g_ref[:, cols]
            for layer in (1, 0):
                resid = (mid_ref if layer else x_ref)[:, cols]
                normed, inv = ln_parts(resid.astype(F32))
                normed_b = normed.astype(BF16)
                act, slope = gelu_both(dot_nn(normed_b, u_ref[layer]))
                grad_pre = (dot_nt(grad, v_ref[layer]) * slope).astype(BF16)
                du_s[layer] += dot_tn(normed_b, grad_pre)
                dv_s[layer] += dot_tn(grad, act.astype(BF16))
                if layer:
                    grad_norm = dot_nt(grad_pre, u_ref[layer])
                    grad = (ln_back(normed, inv, grad_norm) + grad.astype(F32)).astype(BF16)

        @pl.when(tile_id == NT - 1)
        def _():
            du_ref[...] = du_s[...].astype(BF16)
            for layer in range(2):
                dv_ref[layer] = dv_s[layer].T.astype(BF16)

    tile = pl.BlockSpec((TILE, W2), lambda i: (i, 0))
    return pl.pallas_call(
        kernel,
        grid=(NT,),
        in_specs=[tile, tile, tile, whole((2, W1, H1)), whole((2, H1, W1))],
        out_specs=[whole((2, W1, H1)), whole((2, H1, W1))],
        out_shape=[jax.ShapeDtypeStruct((2, W1, H1), BF16), jax.ShapeDtypeStruct((2, H1, W1), BF16)],
        scratch_shapes=[pltpu.VMEM((2, W1, H1), F32), pltpu.VMEM((2, W1, H1), F32)],
        compiler_params=params(),
        name="stage_one_back",
    )(grad_in, x, mid, up_b, down_b)


def head_and_loss(pooled, labels, head_b, global_batch):
    normed, inv = ln_parts(pooled)
    head_in = normed.astype(BF16)
    logits = jnp.dot(head_in, head_b, preferred_element_type=F32)
    probs = jax.nn.softmax(logits, axis=-1)
    class_ids = jnp.arange(logits.shape[1], dtype=jnp.int32)
    onehot = (labels[:, None] == class_ids[None, :]).astype(F32)
    grad_logits = ((probs - onehot) / global_batch).astype(BF16)
    grad_head = dot_tn(head_in, grad_logits).astype(BF16)
    grad_pool = ln_back(normed, inv, dot_nt(grad_logits, head_b)) / PER_IMAGE
    return grad_head, grad_pool.astype(BF16)


def total_sq(grad):
    grad_f = grad.astype(F32)
    return jnp.sum(grad_f * grad_f, axis=(-2, -1))


def solution(mesh):
    data_devs = mesh.shape['data']

    def local_step(x_now, labels_now, x_next, up_one, down_one, merge_proj, up_two, down_two, head_proj, vel_up_one, vel_down_one, vel_merge_proj, vel_up_two, vel_down_two, vel_head_proj):
        images = x_now.shape[0]
        xn = x_now.reshape(ROWS, W2)
        xf = x_next.reshape(ROWS, W2)
        mid, merged, res0, ub1, vb1, mb, su1, sv1, sm = stage_one_now(xn, up_one, down_one, merge_proj)
        res1, ub2, vb2, su2, sv2, pooled = stage_two_now(res0, up_two, down_two)
        grad_head, grad_pool = head_and_loss(pooled[:images], labels_now, head_proj.astype(BF16), images * data_devs)
        grad_pool = jnp.pad(grad_pool, ((0, 128 - images), (0, 0)))
        du2, dv2, dm, grad_mid = stage_two_back(grad_pool, res0, res1, merged, ub2, vb2, mb)
        du1, dv1 = stage_one_back(grad_mid, xn, mid, ub1, vb1)
        du1, dv1, dm, du2, dv2, dh = lax.psum((du1, dv1, dm, du2, dv2, grad_head), 'data')
        sq = lambda folded: jnp.sum(folded, axis=(-2, -1))
        scale = lambda w_sq, g_sq: TRUST * (jnp.sqrt(w_sq) / jnp.sqrt(g_sq))
        scales_one = jnp.concatenate([scale(sq(su1), total_sq(du1)), scale(sq(sv1), total_sq(dv1)), scale(sq(sm), total_sq(dm))[None]])
        scales_two = jnp.concatenate([scale(sq(su2), total_sq(du2)), scale(sq(sv2), total_sq(dv2))])
        res_f, nu1, nv1, nm, qu1, qv1, qm = stage_one_next(xf, scales_one, (up_one, down_one, merge_proj), (vel_up_one, vel_down_one, vel_merge_proj), (du1, dv1, dm))
        nu2, nv2, qu2, qv2, pooled_f = stage_two_next(res_f, scales_two, up_two, down_two, vel_up_two, vel_down_two, du2, dv2)
        nh, qh = lars_block(head_proj, vel_head_proj, dh, scale(jnp.sum(head_proj * head_proj), total_sq(dh)))
        logits = jnp.dot(ln_parts(pooled_f[:images])[0].astype(BF16), nh.astype(BF16), preferred_element_type=F32)
        return logits, nu1, nv1, nm, nu2, nv2, nh, qu1, qv1, qm, qu2, qv2, qh

    batch_split = P('data')
    in_specs = (batch_split,) * 3 + (P(),) * 12
    out_specs = (batch_split,) + (P(),) * 12
    return jax.shard_map(local_step, mesh=mesh, in_specs=in_specs, out_specs=out_specs, check_vma=False)
```

time: 523 us -> 449 us (0.86)
  Pallas kernels: 0 us -> 226 us
  matrix products: 211 us -> 5.31 us
  other arithmetic: 98.1 us -> 22.8 us
  local copies, waits for them, and re-layouts: 37.2 us -> 8.88 us
  waiting for transfers between devices: 150 us -> 161 us
    pallas_call x0 -> x6, Pallas kernels: none -> 226 us  [the longest x1 67.1 us: stage_two_back(): pl.pallas_call(kernel, grid=(2, NCH), in_specs=[whole((128, W2)), act, ac...]
    dot_general x34 -> x4, matrix products: 211 us -> 5.31 us  [the longest x1 2.09 us: head_and_loss(): logits = jnp.dot(head_in, head_b, preferred_element_type=F32)]
    reduce_sum x33 -> x17, other arithmetic: 53.5 us -> 17.2 us  [the longest x6 11.2 us: total_sq(): return jnp.sum(grad_f * grad_f, axis=(-2, -1))]
    another operation x4 -> x0, other arithmetic: 28.5 us -> none
    convert_element_type x6 -> x0, local copies, waits for them, and re-layouts: 17.2 us -> none  [the longest x2 5.38 us: block_forward(): (residual.astype(jnp.float32) + block_out).astype(jnp.bfloat16)]
    psum x1, waiting for transfers between devices: 150 us -> 161 us  [local_step(): lax.psum((du1, dv1, dm, du2, dv2, grad_head), 'data')]
    unnamed x136 -> x24, local copies, waits for them, and re-layouts: 10.8 us -> 0.76 us
    convert_element_type x6 -> x1, other arithmetic: 9.42 us -> 0.08 us  [head_and_loss(): return (grad_head, grad_pool.astype(BF16))]
  transfers between devices with their start and end apart: 1 -> 1, of which waited for: 1 -> 1; matrix products, arithmetic and copies ran while one was open for 4% -> 1% of each run, Pallas kernels for 0% -> 0%
where the time goes in v1:
time: 449 us; the launch traced here: 442 us
  Pallas kernels  226 us (50%)
  waiting for transfers between devices  161 us (36%)
  other arithmetic  22.8 us (5%)
  between operations  17.4 us (4%)
  local copies, waits for them, and re-layouts  8.88 us (2%)
  matrix products  5.31 us (1%)
    psum x1, waiting for transfers between devices, local_step(): lax.psum((du1, dv1, dm, du2, dv2, grad_head), 'data')  161 us
    pallas_call x1, Pallas kernels, stage_two_back(): pl.pallas_call(kernel, grid=(2, NCH), in_specs=[whole((128, W2)), act, ac...  67.1 us
    pallas_call x1, Pallas kernels, stage_two_next(): pl.pallas_call(kernel, grid=(2, NCH), in_specs=[pl.BlockSpec(memory_space...  37.5 us
    pallas_call x1, Pallas kernels, stage_one_back(): pl.pallas_call(kernel, grid=(NT,), in_specs=[tile, tile, tile, whole((2,...  36.3 us
    pallas_call x1, Pallas kernels, stage_two_now(): pl.pallas_call(kernel, grid=(2, NCH), in_specs=[whole((ROWS, W2)), u_spec...  29.9 us
    pallas_call x1, Pallas kernels, stage_one_next(): pl.pallas_call(kernel, grid=(NT,), in_specs=[pl.BlockSpec(memory_space=pl...  28.2 us
    pallas_call x1, Pallas kernels, stage_one_now(): pl.pallas_call(kernel, grid=(NT,), in_specs=[tile, whole((2, W1, H1)), wh...  27.1 us
    reduce_sum x6, other arithmetic, total_sq(): return jnp.sum(grad_f * grad_f, axis=(-2, -1))  11.2 us
  transfers between devices with their start and end apart: 1, of which 1 were waited for; matrix products, arithmetic and copies ran while one was open for 1% of the time, Pallas kernels for 0%

profile of v1, /device:TPU:1, one launch (start us, length us, event | category | flops | bytes accessed | tf_op | source)
XLA Modules:
  0.0 441.8 jit_solution(15443526177479568523)
XLA Ops:
  7.2 3.7 reshape.67.x_ref
  11.0 27.1 %stage_one_now.1 = (bf16[1568,512]{1,0:T(8,128)(2,1)}, bf16[1568,512]{1,0:T(8,128)(2,1)}, bf16[1568,512]{1,0:T(8,128)(2,1)}, bf16[2,128,512]{2,1,0:T(8,128)(2,1)...) custom-call(bf16[1568,512]{1,0:T(8,128)(2,1)} %reshape.67.x_ref, ...), custom_call_target="tpu_custom_call" | custom-call | tf_op jit(solution)/shard_map/stage_one_now/pallas_call | solution.py:127
  38.0 29.9 %stage_two_now.1 = (bf16[1568,512]{1,0:T(8,128)(2,1)}, bf16[2,512,2048]{2,1,0:T(8,128)(2,1)}, bf16[2,2048,512]{2,1,0:T(8,128)(2,1)}, f32[2,8,256]{2,1,0:T(8,128)...) custom-call(bf16[1568,512]{1,0:T(8,128)(2,1)} %get-tuple-element.46.r_ref.r0_ref, f32[2,512,2048]{2,1,0:T(8,128)} %u_ref.7, ...), custom_call_target="tpu_custom_call" | custom-call | tf_op jit(solution)/shard_map/stage_two_now/pallas_call | solution.py:226
  68.0 1.0 slice_reduce_fusion.1
  68.9 0.9 multiply_reduce_fusion.8
  69.9 2.1 fusion.17
  71.9 0.2 fusion.8
  72.2 0.4 fusion.14
  72.6 1.5 convolution_convert_fusion
  74.2 0.7 pad.4.gp_ref
  74.9 67.1 %stage_two_back.1 = (bf16[2,512,2048]{2,1,0:T(8,128)(2,1)}, bf16[2,2048,512]{2,1,0:T(8,128)(2,1)}, bf16[512,512]{1,0:T(8,128)(2,1)}, bf16[1568,512]{1,0:T(8,128)(2,1)}) custom-call(bf16[128,512]{1,0:T(8,128)(2,1)} %pad.4.gp_ref, bf16[1568,512]{1,0:T(8,128)(2,1)} %get-tuple-element.46.r_ref.r0_ref, bf16[1568,512]{1,0:T(8,128)(2,1)} %get-tuple-element.49.r1_ref, ...), custom_call_target="tpu_custom_call" | custom-call | tf_op jit(solution)/shard_map/stage_two_back/pallas_call | solution.py:342
  141.9 36.3 %stage_one_back.1 = (bf16[2,128,512]{2,1,0:T(8,128)(2,1)}, bf16[2,512,128]{2,1,0:T(8,128)(2,1)}) custom-call(bf16[1568,512]{1,0:T(8,128)(2,1)} %get-tuple-element.58.g_ref, bf16[1568,512]{1,0:T(8,128)(2,1)} %reshape.67.x_ref, bf16[1568,512]{1,0:T(8,128)(2,1)} %get-tuple-element.59.mid_ref, bf16[2,128,512]{2,1,0:T(8,128)(2,1)} %get-tuple-element.60.u_ref, ...), custom_call_target="tpu_custom_call" | custom-call | tf_op jit(solution)/shard_map/stage_one_back/pallas_call | solution.py:385
  178.3 0.7 copy-done.7
  179.2 0.6 reduce_sum.184
  180.5 3.7 reshape.68.x_ref
  184.3 0.1 reduce_sum.178
  184.4 1.1 multiply_reduce_fusion.2
  186.3 161.4 %all-reduce.4.cloned.1.call-done = (bf16[512,1000]{0,1:T(8,128)(2,1)}, bf16[2,2048,512]{2,1,0:T(8,128)(2,1)}, bf16[2,512,2048]{2,1,0:T(8,128)(2,1)}, bf16[512,51...) async-done(((bf16[512,1000]{0,1:T(8,128)(2,1)}, bf16[2,2048,512]{2,1,0:T(8,128)(2,1)}, bf16[2,512,2048]{2,1,0:T(8,128)(2,1)}, ...) | async-done | bytes 10461200 | tf_op jit(solution)/shard_map/psum | solution.py:428
  347.7 1.1 multiply_reduce_fusion.5
  348.8 1.1 multiply_reduce_fusion.4
  349.9 1.9 multiply_reduce_fusion.3
  352.5 3.5 multiply_reduce_fusion.1
  356.1 1.2 multiply_reduce_fusion
  357.3 0.7 pad_maximum_fusion.sc_ref
  358.0 0.6 pad_maximum_fusion.1.sc_ref
  358.6 28.2 %stage_one_next.1 = (bf16[1568,512]{1,0:T(8,128)(2,1)}, f32[2,128,512]{2,1,0:T(8,128)}, f32[2,512,128]{2,1,0:T(8,128)}, f32[512,512]{1,0:T(8,128)}, f32[2,128,51...) custom-call(f32[5]{0:T(128)} %pad_maximum_fusion.1.sc_ref, bf16[1568,512]{1,0:T(8,128)(2,1)} %reshape.68.x_ref, ...), custom_call_target="tpu_custom_call" | custom-call | tf_op jit(solution)/shard_map/stage_one_next/pallas_call | solution.py:154
  386.8 37.5 %stage_two_next.1 = (f32[2,512,2048]{2,1,0:T(8,128)}, f32[2,2048,512]{2,1,0:T(8,128)}, f32[2,512,2048]{2,1,0:T(8,128)}, f32[2,2048,512]{2,1,0:T(8,128)}, f32[16,512]{1,0:T(8,128)}) custom-call(f32[4]{0:T(128)} %pad_maximum_fusion.sc_ref, bf16[1568,512]{1,0:T(8,128)(2,1)} %get-tuple-element.67.r_ref, f32[2,512,2048]{2,1,0:T(8,128)} %u_ref.7, ...), custom_call_target="tpu_custom_call" | custom-call | tf_op jit(solution)/shard_map/stage_two_next/pallas_call | solution.py:271
  424.3 0.8 slice_reduce_fusion
  425.1 0.9 multiply_reduce_fusion.6
  426.0 2.4 fusion
  429.1 4.2 fusion.15
  433.3 1.3 fusion.2
  (38 shorter events, 0.6 us)
Async XLA Ops:
  7.2 340.5 %all-reduce.4.cloned.1.call-start = ((), (), s32[]{:S(2)}) async-start(), calls=%async_computation | async-start | bytes 20922368 | tf_op jit(solution)/shard_map/psum | solution.py:428
  67.9 4.2 copy-start
  67.9 4.2 copy-start.4
  67.9 4.2 copy-start.11
  178.2 0.8 copy-start.7
  178.2 0.9 copy-start.10
  178.3 1.0 copy-start.8
  178.3 6.0 %copy-start.9 = (f32[2,8,256]{2,1,0:T(8,128)S(1)}, f32[2,8,256]{2,1,0:T(8,128)}, u32[]{:S(2)}) copy-start(f32[2,8,256]{2,1,0:T(8,128)} %get-tuple-element.47) | copy-start | bytes 49156
  178.3 6.1 %copy-start.6 = (f32[2,8,512]{2,1,0:T(8,128)S(1)}, f32[2,8,512]{2,1,0:T(8,128)}, u32[]{:S(2)}) copy-start(f32[2,8,512]{2,1,0:T(8,128)} %get-tuple-element.55) | copy-start | bytes 98308
  178.3 6.1 %copy-start.1 = (f32[512,1000]{0,1:T(8,128)S(1)}, f32[512,1000]{0,1:T(8,128)}, u32[]{:S(2)}) copy-start(f32[512,1000]{0,1:T(8,128)} %param.23) | copy-start | bytes 6144004
  352.5 3.6 copy-start.2
  429.1 4.2 copy-start.5
  433.3 1.3 copy-start.3
Sparse Core Ops, SparseCore 0:
  178.4 169.2 all-reduce.3

commit v2 on v1

v2 whole, which is shorter than its diff:
```python
import functools

import jax
import jax.numpy as jnp
from jax import lax
from jax.experimental import pallas as pl
from jax.experimental.pallas import tpu as pltpu
from jax.sharding import PartitionSpec as P

MOMENTUM = 0.9
TRUST = 0.1
LN_EPS = 1e-6
GELU_A = 2.0 * 0.7978845608028654
GELU_B = 4.0 * GELU_A * 0.044715
UNIT = 16
LANES = 128
UNIT_SIZE = UNIT * LANES
ROWS = 1568
ROWS_PAD = 1792
PER_IMAGE = 196
W1 = 128
W2 = 512
H1 = 512
H2 = 2048
CHUNK = 512
NCH = H2 // CHUNK
FCHUNK = 1024
NF = H2 // FCHUNK
TILE = 784
NT = ROWS // TILE
TOKENS = 4 * TILE
SPLITS = (784, 784)
HEAD_PAD = 1024
HEAD_ROWS = HEAD_PAD // (2 * NF)
HEAD_UNITS = HEAD_ROWS * W2 // UNIT_SIZE
HERE_AXES = (0, 1)
CHUNK_UNITS = CHUNK * W2 // UNIT_SIZE
F_UNITS = FCHUNK * W2 // UNIT_SIZE
SCALE_SHAPE = (UNIT, LANES)
ONE_SHAPES = [(2, W1, H1), (2, H1, W1), (W2, W2)]
UP_SHAPE, DOWN_SHAPE = (2, W2, H2), (2, H2, W2)
VMEM_LIMIT = 63 * 1024 * 1024
F32 = jnp.float32
BF16 = jnp.bfloat16


def dot_nn(lhs, rhs):
    return lax.dot_general(lhs, rhs, (((1,), (0,)), ((), ())), preferred_element_type=F32)


def dot_nt(lhs, rhs):
    return lax.dot_general(lhs, rhs, (((1,), (1,)), ((), ())), preferred_element_type=F32)


def dot_tn(lhs, rhs):
    return lax.dot_general(lhs, rhs, (((0,), (0,)), ((), ())), preferred_element_type=F32)


def ln_parts(values):
    row_mean = jnp.mean(values, axis=-1, keepdims=True)
    centered = values - row_mean
    variance = jnp.mean(centered * centered, axis=-1, keepdims=True)
    inv = lax.rsqrt(variance + LN_EPS)
    return centered * inv, inv


def ln_back(normed, inv, grad):
    mean_grad = jnp.mean(grad, axis=-1, keepdims=True)
    mean_dot = jnp.mean(grad * normed, axis=-1, keepdims=True)
    return inv * (grad - mean_grad - normed * mean_dot)


def gelu_fwd(half):
    tan = jnp.tanh(half * (GELU_A + GELU_B * (half * half)))
    return half + half * tan


def gelu_both(half):
    sq = half * half
    tan = jnp.tanh(half * (GELU_A + GELU_B * sq))
    above = 1.0 + tan
    return half * above, above * (1.0 + (half * (1.0 - tan)) * (GELU_A + (3.0 * GELU_B) * sq))


def halve(weight):
    return (0.5 * weight).astype(BF16)


def fold_sq(mat):
    rows, cols = mat.shape
    return jnp.sum((mat * mat).reshape(rows // 8, 8, cols), axis=0)


def lars_block(weight, vel, grad, scale):
    new_vel = MOMENTUM * vel + scale * grad.astype(F32)
    return weight - new_vel, new_vel


def put_units(ref, start, mat):
    rows, cols = mat.shape
    groups = rows // UNIT
    for lane in range(cols // LANES):
        ref[pl.ds(start + lane * groups, groups)] = mat[:, lane * LANES:(lane + 1) * LANES].reshape(groups, UNIT, LANES)


def get_units(ref, start, rows, cols):
    groups = rows // UNIT
    parts = [ref[pl.ds(start + lane * groups, groups)].reshape(rows, LANES) for lane in range(cols // LANES)]
    return parts[0] if len(parts) == 1 else jnp.concatenate(parts, axis=1)


struct = jax.ShapeDtypeStruct


def unit_struct(count):
    return struct((count, UNIT, LANES), BF16)


def params(**kwargs):
    return pltpu.CompilerParams(vmem_limit_bytes=VMEM_LIMIT, **kwargs)


def whole(shape):
    zeros = (0,) * len(shape)
    return pl.BlockSpec(shape, lambda *_: zeros)


def token_parts(x_ref, x_s):
    x_s[...] = x_ref[...].astype(F32)
    return [x_s[pl.ds(quarter, TILE, stride=4), :] for quarter in range(4)]


def stage_one_tile(parts, ub, vb, mb):
    outs0, outs1 = [], []
    for resid in parts:
        for layer in range(2):
            normed = ln_parts(resid.astype(F32))[0].astype(BF16)
            act = gelu_fwd(dot_nn(normed, ub[layer])).astype(BF16)
            resid = (resid.astype(F32) + dot_nn(act, vb[layer])).astype(BF16)
            (outs0, outs1)[layer].append(resid)
    mid = jnp.concatenate(outs0, axis=1)
    merged = jnp.concatenate(outs1, axis=1)
    return mid, merged, dot_nn(merged, mb[...]).astype(BF16)


def rows_spec(rows, cols):
    return pl.BlockSpec((rows, cols), lambda i: (i, 0))


def stage_one_now(x, up_one, down_one, merge):
    def kernel(x_ref, u_ref, v_ref, m_ref, mid_ref, merged_ref, res_ref, ub_ref, vb_ref, mb_ref, su_ref, sv_ref, sm_ref, x_s):
        @pl.when(pl.program_id(0) == 0)
        def _():
            ub_ref[...] = halve(u_ref[...])
            vb_ref[...] = v_ref[...].astype(BF16)
            mb_ref[...] = m_ref[...].astype(BF16)
            for layer in range(2):
                su_ref[layer] = fold_sq(u_ref[layer])
                sv_ref[layer] = fold_sq(v_ref[layer])
            sm_ref[...] = fold_sq(m_ref[...])

        mid, merged, res = stage_one_tile(token_parts(x_ref, x_s), ub_ref, vb_ref, mb_ref)
        mid_ref[...] = mid
        merged_ref[...] = merged
        res_ref[...] = res

    tile = rows_spec(TILE, W2)
    act = struct((ROWS, W2), BF16)
    small = [(shape, BF16) for shape in ONE_SHAPES] + [((2, 8, H1), F32), ((2, 8, W1), F32), ((8, W2), F32)]
    return pl.pallas_call(
        kernel,
        grid=(NT,),
        in_specs=[rows_spec(TOKENS, W1)] + [whole(s) for s in ONE_SHAPES],
        out_specs=[tile] * 3 + [whole(s) for s, _ in small],
        out_shape=[act] * 3 + [struct(s, d) for s, d in small],
        scratch_shapes=[pltpu.VMEM((TOKENS, W1), F32)],
        compiler_params=params(),
        name="stage_one_now",
    )(x, up_one, down_one, merge)


def stage_one_next(x, scales, grads, weights, vels):
    def kernel(sc_ref, x_ref, u_ref, v_ref, m_ref, pu_ref, pv_ref, pm_ref, gu_ref, gv_ref, gm_ref, res_ref, nu_ref, nv_ref, nm_ref, qu_ref, qv_ref, qm_ref, ub_ref, vb_ref, mb_ref, x_s):
        @pl.when(pl.program_id(0) == 0)
        def _():
            for layer in range(2):
                nu_ref[layer], qu_ref[layer] = lars_block(u_ref[layer], pu_ref[layer], get_units(gu_ref, 32 * layer, W1, H1), sc_ref[6 + layer:7 + layer, :1])
                nv_ref[layer], qv_ref[layer] = lars_block(v_ref[layer], pv_ref[layer], get_units(gv_ref, 32 * layer, H1, W1), sc_ref[8 + layer:9 + layer, :1])
            nm_ref[...], qm_ref[...] = lars_block(m_ref[...], pm_ref[...], get_units(gm_ref, 0, W2, W2), sc_ref[4:5, :1])
            ub_ref[...] = halve(nu_ref[...])
            vb_ref[...] = nv_ref[...].astype(BF16)
            mb_ref[...] = nm_ref[...].astype(BF16)

        res_ref[...] = stage_one_tile(token_parts(x_ref, x_s), ub_ref, vb_ref, mb_ref)[2]

    shapes = ONE_SHAPES
    units = [pl.BlockSpec((size, 16, 128), lambda i, at=at: (at, 0, 0)) for size, at in ((64, 38), (64, 39), (128, 16))]
    return pl.pallas_call(
        kernel,
        grid=(NT,),
        in_specs=[whole(SCALE_SHAPE), rows_spec(TOKENS, W1)] + [whole(s) for s in shapes] * 2 + units,
        out_specs=[rows_spec(TILE, W2)] + [whole(s) for s in shapes] * 2,
        out_shape=[struct((ROWS, W2), BF16)] + [struct(s, F32) for s in shapes] * 2,
        scratch_shapes=[pltpu.VMEM(s, BF16) for s in shapes] + [pltpu.VMEM((TOKENS, W1), F32)],
        compiler_params=params(),
        name="stage_one_next",
    )(scales, x, *weights, *vels, grads, grads, grads)


def row_parts():
    return [(sum(SPLITS[:index]), size) for index, size in enumerate(SPLITS)]


def stage_two_start(chunk, src_ref, dst_norm, acc_ref):
    for start, size in row_parts():
        resid = src_ref[start:start + size].astype(F32)
        dst_norm[start:start + size] = ln_parts(resid)[0].astype(BF16)
        acc_ref[start:start + size] = resid


def stage_two_step(norm_ref, acc_ref, ub, vb):
    for start, size in row_parts():
        act = gelu_fwd(dot_nn(norm_ref[start:start + size], ub)).astype(BF16)
        acc_ref[start:start + size] += dot_nn(act, vb)


def pool_images(resid_ref):
    cols = lax.broadcasted_iota(jnp.int32, (16, ROWS_PAD), 1)
    base = lax.broadcasted_iota(jnp.int32, (16, ROWS_PAD), 0) * PER_IMAGE
    mask = ((cols >= base) & (cols < base + PER_IMAGE) & (cols < ROWS)).astype(F32).astype(BF16)
    return dot_nn(mask, resid_ref[...]) * (1.0 / PER_IMAGE)


def head_block(layer, chunk, h_ref, classes):
    at = pl.multiple_of((layer * NF + chunk) * HEAD_ROWS, HEAD_ROWS)
    rows = at + lax.broadcasted_iota(jnp.int32, h_ref.shape, 0)
    return at, jnp.where(rows < classes, h_ref[...], 0.0)


def two_specs():
    u_spec = pl.BlockSpec((1, W2, FCHUNK), lambda l, j: (l, 0, j))
    v_spec = pl.BlockSpec((1, FCHUNK, W2), lambda l, j: (l, j, 0))
    return u_spec, v_spec, pl.BlockSpec((HEAD_ROWS, W2), lambda l, j: (l * NF + j, 0))


def by_layer(layer, chunk):
    return layer, 0, 0


def stage_two_now(res_in, labels, up_two, down_two, head, global_batch):
    classes = head.shape[0]
    images = labels.shape[0]

    def kernel(r_ref, lab_ref, u_ref, v_ref, h_ref, mid_ref, ub_ref, vb_ref, su_ref, sv_ref, sh_ref, dh_ref, gp_ref, norm_s, acc_s, res_s, hb_s):
        layer, chunk = pl.program_id(0), pl.program_id(1)

        @pl.when((layer == 0) & (chunk == 0))
        def _():
            sh_ref[...] = jnp.zeros_like(sh_ref)

        @pl.when(chunk == 0)
        def _():
            @pl.when(layer == 0)
            def _():
                stage_two_start(chunk, r_ref, norm_s, acc_s)

            @pl.when(layer == 1)
            def _():
                stage_two_start(chunk, mid_ref, norm_s, acc_s)
            su_ref[...] = jnp.zeros_like(su_ref)
            sv_ref[...] = jnp.zeros_like(sv_ref)

        ub = halve(u_ref[0])
        vb = v_ref[0].astype(BF16)
        ub_ref[0] = ub
        vb_ref[0] = halve(v_ref[0])
        su_ref[0] += fold_sq(u_ref[0])
        sv_ref[0] += fold_sq(v_ref[0])
        at, head_part = head_block(layer, chunk, h_ref, classes)
        sh_ref[...] += fold_sq(head_part)
        hb_s[pl.ds(at, HEAD_ROWS)] = head_part.astype(BF16)
        stage_two_step(norm_s, acc_s, ub, vb)

        @pl.when((chunk == NF - 1) & (layer == 0))
        def _():
            mid_ref[...] = acc_s[...].astype(BF16)

        @pl.when((chunk == NF - 1) & (layer == 1))
        def _():
            res_s[:ROWS] = acc_s[...].astype(BF16)
            res_s[ROWS:] = jnp.zeros((ROWS_PAD - ROWS, W2), BF16)
            normed, inv = ln_parts(pool_images(res_s))
            head_in = normed.astype(BF16)
            logits = dot_nt(head_in, hb_s[...])
            cols = lax.broadcasted_iota(jnp.int32, logits.shape, 1)
            rows = lax.broadcasted_iota(jnp.int32, logits.shape, 0)
            live = cols < classes
            top = jnp.max(jnp.where(live, logits, -jnp.inf), axis=-1, keepdims=True)
            expd = jnp.where(live, jnp.exp(logits - top), 0.0)
            probs = expd / jnp.sum(expd, axis=-1, keepdims=True)
            onehot = (cols == lab_ref[...]).astype(F32)
            grad_logits = jnp.where(rows < images, (probs - onehot) / global_batch, 0.0).astype(BF16)
            grad_head = dot_tn(grad_logits, head_in).astype(BF16)
            for block in range(2 * NF):
                put_units(dh_ref, block * HEAD_UNITS, grad_head[block * HEAD_ROWS:(block + 1) * HEAD_ROWS])
            grad_pool = ln_back(normed, inv, dot_nn(grad_logits, hb_s[...])) / PER_IMAGE
            gp_ref[...] = jnp.zeros_like(gp_ref)
            gp_ref[:16] = grad_pool.astype(BF16)

    u_spec, v_spec, h_spec = two_specs()
    return pl.pallas_call(
        kernel,
        grid=(2, NF),
        in_specs=[whole((ROWS, W2)), whole((16, 1)), u_spec, v_spec, h_spec],
        out_specs=[whole((ROWS, W2)), u_spec, v_spec, pl.BlockSpec((1, 8, FCHUNK), by_layer), pl.BlockSpec((1, 8, W2), by_layer), whole((8, W2)), whole((256, UNIT, LANES)), whole((LANES, W2))],
        out_shape=[struct((ROWS, W2), BF16), struct(UP_SHAPE, BF16), struct(DOWN_SHAPE, BF16), struct((2, 8, FCHUNK), F32), struct((2, 8, W2), F32), struct((8, W2), F32), unit_struct(256), struct((LANES, W2), BF16)],
        scratch_shapes=[pltpu.VMEM((ROWS, W2), BF16), pltpu.VMEM((ROWS, W2), F32), pltpu.VMEM((ROWS_PAD, W2), BF16), pltpu.VMEM((HEAD_PAD, W2), BF16)],
        compiler_params=params(),
        name="stage_two_now",
    )(res_in, jnp.pad(labels, (0, 16 - images))[:, None], up_two, down_two, head)


def stage_two_next(res_in, scales, grads, weights, vels, images):
    classes = weights[2].shape[0]

    def kernel(sc_ref, r_ref, u_ref, v_ref, h_ref, pu_ref, pv_ref, ph_ref, gu_ref, gv_ref, gh_ref, nu_ref, nv_ref, nh_ref, qu_ref, qv_ref, qh_ref, out_ref, norm_s, acc_s, res_s, hb_s):
        layer, chunk = pl.program_id(0), pl.program_id(1)

        @pl.when(chunk == 0)
        def _():
            @pl.when(layer == 0)
            def _():
                stage_two_start(chunk, r_ref, norm_s, acc_s)

            @pl.when(layer == 1)
            def _():
                stage_two_start(chunk, res_s, norm_s, acc_s)

        new_u, qu_ref[0] = lars_block(u_ref[0], pu_ref[0], get_units(gu_ref, 0, W2, FCHUNK), sc_ref[pl.ds(layer, 1), :1])
        nu_ref[0] = new_u
        for part in range(FCHUNK // CHUNK):
            rows = slice(part * CHUNK, (part + 1) * CHUNK)
            nv_ref[0, rows], qv_ref[0, rows] = lars_block(v_ref[0, rows], pv_ref[0, rows], get_units(gv_ref, part * CHUNK_UNITS, CHUNK, W2), sc_ref[pl.ds(2 + layer, 1), :1])
        nh_ref[...], qh_ref[...] = lars_block(h_ref[...], ph_ref[...], get_units(gh_ref, 0, HEAD_ROWS, W2), sc_ref[5:6, :1])
        at, head_part = head_block(layer, chunk, nh_ref, classes)
        hb_s[pl.ds(at, HEAD_ROWS)] = head_part.astype(BF16)
        stage_two_step(norm_s, acc_s, halve(new_u), nv_ref[0].astype(BF16))

        @pl.when(chunk == NF - 1)
        def _():
            res_s[:ROWS] = acc_s[...].astype(BF16)

            @pl.when(layer == 1)
            def _():
                res_s[ROWS:] = jnp.zeros((ROWS_PAD - ROWS, W2), BF16)
                head_in = ln_parts(pool_images(res_s))[0].astype(BF16)
                out_ref[...] = dot_nt(head_in, hb_s[...])[:images, :classes]

    u_spec, v_spec, h_spec = two_specs()
    units = [pl.BlockSpec((size, UNIT, LANES), lambda l, j, base=base // size: (base + l * NF + j, 0, 0)) for size, base in ((F_UNITS, 0), (F_UNITS, 1024), (HEAD_UNITS, 2176))]
    return pl.pallas_call(
        kernel,
        grid=(2, NF),
        in_specs=[whole(SCALE_SHAPE), whole((ROWS, W2))] + [u_spec, v_spec, h_spec] * 2 + units,
        out_specs=[u_spec, v_spec, h_spec] * 2 + [whole((images, classes))],
        out_shape=[struct(UP_SHAPE, F32), struct(DOWN_SHAPE, F32), struct((classes, W2), F32)] * 2 + [struct((images, classes), F32)],
        scratch_shapes=[pltpu.VMEM((ROWS, W2), BF16), pltpu.VMEM((ROWS, W2), F32), pltpu.VMEM((ROWS_PAD, W2), BF16), pltpu.VMEM((HEAD_PAD, W2), BF16)],
        compiler_params=params(),
        name="stage_two_next",
    )(scales, res_in, *weights, *vels, grads, grads, grads)


def stage_two_back(grad_pool, res_in, res_mid, merged, up_b, down_b, merge_b):
    def kernel(gp_ref, r0_ref, r1_ref, m_ref, u_ref, v_ref, mw_ref, du_ref, dv_ref, dm_ref, gout_ref, g_s, gt_s, n_s, nt_s, act_s, pre_s, dn_s):
        step, chunk = pl.program_id(0), pl.program_id(1)

        @pl.when((step == 0) & (chunk == 0))
        def _():
            rows = lax.broadcasted_iota(jnp.int32, (ROWS, 128), 0)
            base = lax.broadcasted_iota(jnp.int32, (ROWS, 128), 1) * PER_IMAGE
            mask = ((rows >= base) & (rows < base + PER_IMAGE)).astype(F32).astype(BF16)
            g_s[...] = dot_nn(mask, gp_ref[...]).astype(BF16)
            gt_s[...] = jnp.zeros_like(gt_s)
            nt_s[...] = jnp.zeros_like(nt_s)
            gt_s[:, :ROWS] = g_s[...].T
            act_s[ROWS:] = jnp.zeros((ROWS_PAD - ROWS, CHUNK), BF16)
            pre_s[ROWS:] = jnp.zeros((ROWS_PAD - ROWS, CHUNK), BF16)

        def begin(src_ref):
            n_s[...] = ln_parts(src_ref[...].astype(F32))[0].astype(BF16)
            nt_s[:, :ROWS] = n_s[...].T
            dn_s[...] = jnp.zeros_like(dn_s)

        @pl.when((step == 0) & (chunk == 0))
        def _():
            begin(r1_ref)

        @pl.when((step == 1) & (chunk == 0))
        def _():
            begin(r0_ref)

        ub = u_ref[0]
        vb = v_ref[0]
        for start, size in row_parts():
            act, slope = gelu_both(dot_nn(n_s[start:start + size], ub))
            grad_pre = (dot_nt(g_s[start:start + size], vb) * slope).astype(BF16)
            act_s[start:start + size] = act.astype(BF16)
            pre_s[start:start + size] = grad_pre
            dn_s[start:start + size] += dot_nt(grad_pre, ub)
        put_units(du_ref, 0, dot_nn(nt_s[...], pre_s[...]).astype(BF16))
        put_units(dv_ref, 0, dot_nn(gt_s[...], act_s[...]).T.astype(BF16))

        def finish(src_ref):
            normed, inv = ln_parts(src_ref[...].astype(F32))
            g_s[...] = (ln_back(normed, inv + inv, dn_s[...]) + g_s[...].astype(F32)).astype(BF16)

        @pl.when((step == 0) & (chunk == NCH - 1))
        def _():
            finish(r1_ref)
            gt_s[:, :ROWS] = g_s[...].T

        @pl.when((step == 1) & (chunk == NCH - 1))
        def _():
            finish(r0_ref)
            gout_ref[...] = dot_nt(g_s[...], mw_ref[...]).astype(BF16)
            put_units(dm_ref, 0, dot_tn(m_ref[...], g_s[...]).astype(BF16))

    u_spec = pl.BlockSpec((1, W2, CHUNK), lambda l, j: (1 - l, 0, j))
    v_spec = pl.BlockSpec((1, CHUNK, W2), lambda l, j: (1 - l, j, 0))
    g_spec = pl.BlockSpec((CHUNK_UNITS, UNIT, LANES), lambda l, j: ((1 - l) * NCH + j, 0, 0))
    act = whole((ROWS, W2))
    return pl.pallas_call(
        kernel,
        grid=(2, NCH),
        in_specs=[whole((128, W2)), act, act, act, u_spec, v_spec, whole((W2, W2))],
        out_specs=[g_spec, g_spec, whole((128, UNIT, LANES)), act],
        out_shape=[unit_struct(1024), unit_struct(1024), unit_struct(128), struct((ROWS, W2), BF16)],
        scratch_shapes=[pltpu.VMEM((ROWS, W2), BF16), pltpu.VMEM((W2, ROWS_PAD), BF16), pltpu.VMEM((ROWS, W2), BF16), pltpu.VMEM((W2, ROWS_PAD), BF16), pltpu.VMEM((ROWS_PAD, CHUNK), BF16), pltpu.VMEM((ROWS_PAD, CHUNK), BF16), pltpu.VMEM((ROWS, W2), F32)],
        compiler_params=params(),
        name="stage_two_back",
    )(grad_pool, res_in, res_mid, merged, up_b, down_b, merge_b)


def stage_one_back(grad_in, x, mid, up_b, down_b):
    def kernel(g_ref, x_ref, mid_ref, u_ref, v_ref, du_ref, dv_ref, du_s, dv_s, x_s, vh_s):
        tile_id = pl.program_id(0)

        @pl.when(tile_id == 0)
        def _():
            du_s[...] = jnp.zeros_like(du_s)
            dv_s[...] = jnp.zeros_like(dv_s)
            vh_s[...] = halve(v_ref[...].astype(F32))

        for quarter, start in enumerate(token_parts(x_ref, x_s)):
            cols = slice(quarter * W1, (quarter + 1) * W1)
            grad = g_ref[:, cols]
            for layer in (1, 0):
                normed, inv = ln_parts(mid_ref[:, cols].astype(F32) if layer else start)
                normed_b = normed.astype(BF16)
                act, slope = gelu_both(dot_nn(normed_b, u_ref[layer]))
                grad_pre = (dot_nt(grad, vh_s[layer]) * slope).astype(BF16)
                du_s[layer] += dot_tn(normed_b, grad_pre)
                dv_s[layer] += dot_tn(grad, act.astype(BF16))
                if layer:
                    grad_norm = dot_nt(grad_pre, u_ref[layer])
                    grad = (ln_back(normed, inv + inv, grad_norm) + grad.astype(F32)).astype(BF16)

        @pl.when(tile_id == NT - 1)
        def _():
            for layer in range(2):
                put_units(du_ref, 32 * layer, du_s[layer].astype(BF16))
                put_units(dv_ref, 32 * layer, dv_s[layer].T.astype(BF16))

    tile = rows_spec(TILE, W2)
    return pl.pallas_call(
        kernel,
        grid=(NT,),
        in_specs=[tile, rows_spec(TOKENS, W1), tile] + [whole(s) for s in ONE_SHAPES[:2]],
        out_specs=[whole((64, UNIT, LANES))] * 2,
        out_shape=[unit_struct(64)] * 2,
        scratch_shapes=[pltpu.VMEM(ONE_SHAPES[0], F32), pltpu.VMEM(ONE_SHAPES[0], F32), pltpu.VMEM((TOKENS, W1), F32), pltpu.VMEM(ONE_SHAPES[1], BF16)],
        compiler_params=params(),
        name="stage_one_back",
    )(grad_in, x, mid, up_b, down_b)


AXIS_STEP = (2, 8, 32)
STREAM_UNITS = (14, 14, 13, 13, 13, 13)
HALF = 1280
TOTAL = 2 * HALF
COUNTS = (512,) * 4 + (128, 256) + (32,) * 4
SEGMENTS = (1024, 1024, 128, 256, 64, 64)


def stream_plan():
    plan, base, slot = [], 0, 0
    for index, units in enumerate(STREAM_UNITS):
        order, sub = index // 2, index % 2
        axes = [(order + shift) % 3 for shift in range(3)]
        hops = [(axis, (sub + turn) % 2) for axis in axes for turn in range(2)]
        plan.append((units, base, slot, hops))
        base += 16 * units
        slot += 17 * units
    return plan, slot


def sum_grads(parts, squares):
    plan, slot_units = stream_plan()
    count = len(plan)

    def kernel(*refs):
        part_refs, sq_refs = refs[:6], refs[6:12]
        out_ref, scale_ref, flat, pair_buf, slots, load_sem, out_sem, pair_send, pair_recv, back_send, back_recv, hop_send, hop_recv, ready = refs[12:]
        me = lax.axis_index('data')
        core = lax.rem(me, 2)
        peer = me + 1 - 2 * core
        mine = core * HALF
        theirs = (1 - core) * HALF
        spots = [lax.rem(me // step, 4) for step in AXIS_STEP]
        partner, bit = {}, {}
        for axis in range(3):
            spot = spots[axis]
            partner[axis, 0] = me + (1 - 2 * lax.rem(spot, 2)) * AXIS_STEP[axis]
            partner[axis, 1] = me + (3 - 2 * spot) * AXIS_STEP[axis]
            bit[axis, 0] = lax.rem((spot + 1) // 2, 2)
            bit[axis, 1] = spot // 2

        loads = [pltpu.make_async_copy(part_refs[k], flat.at[pl.ds(sum(SEGMENTS[:k]), size)], load_sem.at[k]) for k, size in enumerate(SEGMENTS)]
        for load in loads:
            load.start()
        barrier = pltpu.get_barrier_semaphore()
        for other in [peer] + list(partner.values()):
            pl.semaphore_signal(barrier, inc=1, device_id=(other,), device_id_type=pl.DeviceIdType.MESH)
        pl.semaphore_wait(barrier, 7)
        for load in loads:
            load.wait()

        def send(src, dst, send_sem, recv_sem, device):
            copy = pltpu.make_async_remote_copy(src_ref=src, dst_ref=dst, send_sem=send_sem, recv_sem=recv_sem, device_id=(device,), device_id_type=pl.DeviceIdType.MESH)
            copy.start()
            return copy

        def add_in(start, src, src_start, units, blocks):
            def body(index, carry):
                at = pl.ds(start + index * units, units)
                flat[at] = flat[at] + src[pl.ds(src_start + index * units, units)]
                return carry
            lax.fori_loop(0, blocks, body, 0)

        pairs = [send(flat.at[pl.ds(theirs + base, 16 * units)], pair_buf.at[pl.ds(base, 16 * units)], pair_send.at[k], pair_recv.at[k], peer) for k, (units, base, slot, hops) in enumerate(plan)]
        held = [mine + base for units, base, slot, hops in plan]
        kept, gone = [[] for _ in plan], [[] for _ in plan]
        for k, (units, base, slot, hops) in enumerate(plan):
            start = held[k]
            for turn in range(4):
                size = (8 >> turn) * units
                flag = bit[hops[turn]]
                gone[k].append(start + (1 - flag) * size)
                start = start + flag * size
                kept[k].append(start)
        copies = {}

        def slot_at(k, turn):
            units, slot = plan[k][0], plan[k][2]
            return slot + sum((8 >> t) if t < 4 else 1 for t in range(turn)) * units

        def hop(k, turn):
            units, hops = plan[k][0], plan[k][3]
            size = (8 >> turn) * units if turn < 4 else units
            src = gone[k][turn] if turn < 4 else kept[k][3]
            copies[k, turn] = send(flat.at[pl.ds(src, size)], slots.at[pl.ds(slot_at(k, turn), size)], hop_send.at[k, turn], hop_recv.at[k, turn], partner[hops[turn]])

        for k in range(count):
            units, base = plan[k][:2]
            pairs[k].wait_recv()
            add_in(gone[k][0], pair_buf, gone[k][0] - mine, units, 8)
            hop(k, 0)
            add_in(kept[k][0], pair_buf, kept[k][0] - mine, units, 8)
        def tell(k, turn, device):
            pl.semaphore_signal(ready.at[k, turn], inc=1, device_id=(device,), device_id_type=pl.DeviceIdType.MESH)

        for turn in range(6):
            if turn == 5:
                for k in range(count):
                    pairs[k].wait_send()
                    tell(k, 4, peer)
                    for early in range(4):
                        copies[k, early].wait_send()
                        tell(k, early, partner[plan[k][3][early]])
            for k in range(count):
                units = plan[k][0]
                copies[k, turn].wait_recv()
                if turn < 3:
                    blocks = 4 >> turn
                    for dst in (gone[k][turn + 1], kept[k][turn + 1]):
                        add_in(dst, slots, slot_at(k, turn) + dst - kept[k][turn], units, blocks)
                        if dst is gone[k][turn + 1]:
                            hop(k, turn + 1)
                else:
                    if turn > 3:
                        copies[k, turn].wait_send()
                    add_in(kept[k][3], slots, slot_at(k, turn), units, 1)
                    if turn < 5:
                        hop(k, turn + 1)
        outs = []

        def share(k, turn):
            units, hops = plan[k][0], plan[k][3]
            region = pl.ds(kept[k][turn], (8 >> turn) * units)
            pl.semaphore_wait(ready.at[k, turn], 1)
            copies[k, 9 - turn] = send(flat.at[region], flat.at[region], hop_send.at[k, 9 - turn], hop_recv.at[k, 9 - turn], partner[hops[turn]])

        def put(region, index):
            copy = pltpu.make_async_copy(flat.at[region], out_ref.at[region], out_sem.at[index])
            copy.start()
            outs.append(copy)

        backs = {}
        for k in range(count):
            share(k, 3)
        for turn in (3, 2, 1, 0):
            for k in range(count):
                units = plan[k][0]
                copies[k, 9 - turn].wait_recv()
                if turn:
                    share(k, turn - 1)
                if turn < 2:
                    region = pl.ds(kept[k][0] if turn else gone[k][0], 8 * units)
                    if turn:
                        pl.semaphore_wait(ready.at[k, 4], 1)
                    backs[k, turn] = send(flat.at[region], flat.at[region], back_send.at[k, turn], back_recv.at[k, turn], peer)
                    put(region, 4 * k + turn)
        for k in range(count):
            for turn in (1, 0):
                backs[k, turn].wait_recv()
            put(pl.ds(theirs + plan[k][1], 16 * plan[k][0]), 4 * k + 2)
        squares = [ref.at[row] for ref in sq_refs for row in range(ref.shape[0])]
        for index, size in enumerate(COUNTS):
            def body(step, total, first=sum(COUNTS[:index])):
                block = flat[pl.ds(first + step * UNIT, UNIT)].astype(F32)
                return total + jnp.sum(block * block, axis=HERE_AXES, keepdims=True)[0]
            grad_sq = jnp.sum(lax.fori_loop(0, size // UNIT, body, jnp.zeros((1, LANES), F32)), axis=-1, keepdims=True)
            weight_sq = jnp.sum(jnp.sum(squares[index][...], axis=0, keepdims=True), axis=-1, keepdims=True)
            scale_ref[pl.ds(index, 1), :] = jnp.broadcast_to(TRUST * (jnp.sqrt(weight_sq) / jnp.sqrt(grad_sq)), (1, LANES))
        for copy in outs:
            copy.wait()
        for k in range(count):
            for turn in (1, 0):
                backs[k, turn].wait_send()
            for turn in range(6, 10):
                copies[k, turn].wait_send()

    anywhere = pl.BlockSpec(memory_space=pl.ANY)
    vmem = pl.BlockSpec(memory_space=pltpu.VMEM)
    dma = pltpu.SemaphoreType.DMA
    return pl.pallas_call(
        kernel,
        in_specs=[anywhere] * 6 + [vmem] * 6,
        out_specs=[anywhere, vmem],
        out_shape=[unit_struct(TOTAL), struct(SCALE_SHAPE, F32)],
        scratch_shapes=[pltpu.VMEM((TOTAL, UNIT, LANES), BF16), pltpu.VMEM((HALF, UNIT, LANES), BF16), pltpu.VMEM((slot_units, UNIT, LANES), BF16), dma((6,)), dma((4 * count,)), dma((count,)), dma((count,)), dma((count, 2)), dma((count, 2)), dma((count, 10)), dma((count, 10)), pltpu.SemaphoreType.REGULAR((count, 5))],
        compiler_params=params(collective_id=0, has_side_effects=True),
        name="sum_grads",
    )(*parts, *squares)


def solution(mesh):
    data_devs = mesh.shape['data']

    def local_step(x_now, labels_now, x_next, up_one, down_one, merge_proj, up_two, down_two, head_proj, vel_up_one, vel_down_one, vel_merge_proj, vel_up_two, vel_down_two, vel_head_proj):
        images = x_now.shape[0]
        xn = x_now.reshape(4 * ROWS, W1)
        xf = x_next.reshape(4 * ROWS, W1)
        mid, merged, res0, ub1, vb1, mb, su1, sv1, sm = stage_one_now(xn, up_one, down_one, merge_proj)
        res1, ub2, vb2, su2, sv2, sh, dh, grad_pool = stage_two_now(res0, labels_now, up_two, down_two, head_proj.T, images * data_devs)
        du2, dv2, dm, grad_mid = stage_two_back(grad_pool, res0, res1, merged, ub2, vb2, mb)
        du1, dv1 = stage_one_back(grad_mid, xn, mid, ub1, vb1)
        grads, scales = sum_grads((du2, dv2, dm, dh, du1, dv1), (su2, sv2, sm[None], sh[None], su1, sv1))
        res_f, nu1, nv1, nm, qu1, qv1, qm = stage_one_next(xf, scales, grads, (up_one, down_one, merge_proj), (vel_up_one, vel_down_one, vel_merge_proj))
        nu2, nv2, nh, qu2, qv2, qh, logits = stage_two_next(res_f, scales, grads, (up_two, down_two, head_proj.T), (vel_up_two, vel_down_two, vel_head_proj.T), images)
        return logits, nu1, nv1, nm, nu2, nv2, nh.T, qu1, qv1, qm, qu2, qv2, qh.T

    batch_split = P('data')
    in_specs = (batch_split,) * 3 + (P(),) * 12
    out_specs = (batch_split,) + (P(),) * 12
    return jax.shard_map(local_step, mesh=mesh, in_specs=in_specs, out_specs=out_specs, check_vma=False)
```

time: 449 us -> 280 us (0.62)
  waiting for transfers between devices: 161 us -> 0 us
  Pallas kernels: 226 us -> 273 us
  other arithmetic: 22.8 us -> 0 us
  between operations: 17.4 us -> 0.89 us
  local copies, waits for them, and re-layouts: 8.88 us -> 1.34 us
  matrix products: 5.31 us -> 0 us
    psum x1 -> x0, waiting for transfers between devices: 161 us -> none  [local_step(): lax.psum((du1, dv1, dm, du2, dv2, grad_head), 'data')]
    pallas_call x5 -> x6, Pallas kernels: 159 us -> 215 us  [the longest x1 90.7 us: sum_grads(): pl.pallas_call(kernel, in_specs=[anywhere] * 6 + [vmem] * 6, out_specs=[a...]
    reduce_sum x17 -> x0, other arithmetic: 17.2 us -> none  [the longest x6 11.2 us: total_sq(): return jnp.sum(grad_f * grad_f, axis=(-2, -1))]
    pallas_call x1, Pallas kernels: 67.1 us -> 57.8 us  [stage_two_back(): pl.pallas_call(kernel, grid=(2, NCH), in_specs=[whole((128, W2)), act, ac...]
    reshape x2 -> x0, local copies, waits for them, and re-layouts: 7.46 us -> none  [the longest x1 3.73 us: local_step(): xf = x_next.reshape(ROWS, W2)]
    dot_general x4 -> x0, matrix products: 5.31 us -> none  [the longest x1 2.09 us: head_and_loss(): logits = jnp.dot(head_in, head_b, preferred_element_type=F32)]
  transfers between devices with their start and end apart: 1 -> 0, of which waited for: 1 -> 0; matrix products, arithmetic and copies ran while one was open for 1% -> 0% of each run, Pallas kernels for 0% -> 0%
where the time goes in v2:
time: 280 us; the launch traced here: 275 us
  Pallas kernels  273 us (98%)
    pallas_call x1, Pallas kernels, sum_grads(): pl.pallas_call(kernel, in_specs=[anywhere] * 6 + [vmem] * 6, out_specs=[a...  90.7 us
    pallas_call x1, Pallas kernels, stage_two_back(): pl.pallas_call(kernel, grid=(2, NCH), in_specs=[whole((128, W2)), act, ac...  57.8 us
    pallas_call x1, Pallas kernels, stage_two_next(): pl.pallas_call(kernel, grid=(2, NF), in_specs=[whole(SCALE_SHAPE), whole(...  34.9 us
    pallas_call x1, Pallas kernels, stage_one_back(): pl.pallas_call(kernel, grid=(NT,), in_specs=[tile, rows_spec(TOKENS, W1),...  27.9 us
    pallas_call x1, Pallas kernels, stage_two_now(): pl.pallas_call(kernel, grid=(2, NF), in_specs=[whole((ROWS, W2)), whole((...  26.5 us
    pallas_call x1, Pallas kernels, stage_one_next(): pl.pallas_call(kernel, grid=(NT,), in_specs=[whole(SCALE_SHAPE), rows_spe...  18 us
    pallas_call x1, Pallas kernels, stage_one_now(): pl.pallas_call(kernel, grid=(NT,), in_specs=[rows_spec(TOKENS, W1)] + [wh...  16.9 us

profile of v2, /device:TPU:1, one launch (start us, length us, event | category | flops | bytes accessed | tf_op | source)
XLA Modules:
  0.0 274.9 jit_solution(17984543708630662867)
XLA Ops:
  0.6 0.7 pad_bitcast_fusion
  1.3 0.7 copy.28.lab_ref
  2.0 16.9 %stage_one_now.1 = (bf16[1568,512]{1,0:T(8,128)(2,1)}, bf16[1568,512]{1,0:T(8,128)(2,1)}, bf16[1568,512]{1,0:T(8,128)(2,1)}, bf16[2,128,512]{2,1,0:T(8,128)(2,1)...) custom-call(bf16[6272,128]{1,0:T(8,128)(2,1)} %bitcast.12, ...), custom_call_target="tpu_custom_call" | custom-call | tf_op jit(solution)/shard_map/stage_one_now/pallas_call | solution.py:170
  18.9 26.5 %stage_two_now.1 = (bf16[1568,512]{1,0:T(8,128)(2,1)}, bf16[2,512,2048]{2,1,0:T(8,128)(2,1)}, bf16[2,2048,512]{2,1,0:T(8,128)(2,1)}, f32[2,8,1024]{2,1,0:T(8,128...) custom-call(bf16[1568,512]{1,0:T(8,128)(2,1)} %get-tuple-element.52.r_ref, ...), custom_call_target="tpu_custom_call" | custom-call | tf_op jit(solution)/shard_map/stage_two_now/pallas_call | solution.py:311
  45.3 57.8 %stage_two_back.1 = (bf16[1024,16,128]{2,1,0:T(8,128)(2,1)}, bf16[1024,16,128]{2,1,0:T(8,128)(2,1)}, bf16[128,16,128]{2,1,0:T(8,128)(2,1)}, bf16[1568,512]{1,0:T(8,128)(2,1)}) custom-call(bf16[128,512]{1,0:T(8,128)(2,1)} %get-tuple-element.53.gp_ref, bf16[1568,512]{1,0:T(8,128)(2,1)} %get-tuple-element.52.r_ref.r0_ref, ...), custom_call_target="tpu_custom_call" | custom-call | tf_op jit(solution)/shard_map/stage_two_back/pallas_call | solution.py:432
  103.2 27.9 %stage_one_back.1 = (bf16[64,16,128]{2,1,0:T(8,128)(2,1)}, bf16[64,16,128]{2,1,0:T(8,128)(2,1)}) custom-call(bf16[1568,512]{1,0:T(8,128)(2,1)} %get-tuple-element.63.g_ref, bf16[6272,128]{1,0:T(8,128)(2,1)} %bitcast.13, bf16[1568,512]{1,0:T(8,128)(2,1)} %get-tuple-element.64.mid_ref, bf16[2,128,512]{2,1,0:T(8,128)(2,1)} %get-tuple-element.65.u_ref, ...), custom_call_target="tpu_custom_call" | custom-call | tf_op jit(solution)/shard_map/stage_one_back/pallas_call | solution.py:475
  131.0 90.7 %sum_grads.1 = (bf16[2560,16,128]{2,1,0:T(8,128)(2,1)}, f32[16,128]{1,0:T(8,128)}) custom-call(bf16[1024,16,128]{2,1,0:T(8,128)(2,1)} %get-tuple-element.59.refs_0_, bf16[1024,16,128]{2,1,0:T(8,128)(2,1)} %get-tuple-element.60.refs_1_, bf16[128,16,128]{2,1,0:T(8,128)(2,1)} %get-tuple-element.61.refs_2_, bf16[256,16,128]{2,1,0:T(8,128)(2,1)} %get-tuple-element.62.refs_3_, ...), custom_call_target="tpu_custom_call" | custom-call | tf_op jit(solution)/shard_map/sum_grads/pallas_call | solution.py:656
  221.8 18.0 %stage_one_next.1 = (bf16[1568,512]{1,0:T(8,128)(2,1)}, f32[2,128,512]{2,1,0:T(8,128)}, f32[2,512,128]{2,1,0:T(8,128)}, f32[512,512]{1,0:T(8,128)}, f32[2,128,51...) custom-call(f32[16,128]{1,0:T(8,128)} %get-tuple-element.75.sc_ref, bf16[6272,128]{1,0:T(8,128)(2,1)} %bitcast.15, ...), custom_call_target="tpu_custom_call" | custom-call | tf_op jit(solution)/shard_map/stage_one_next/pallas_call | solution.py:198
  239.8 34.9 %stage_two_next.1 = (f32[2,512,2048]{2,1,0:T(8,128)}, f32[2,2048,512]{2,1,0:T(8,128)}, f32[1000,512]{1,0:T(8,128)}, f32[2,512,2048]{2,1,0:T(8,128)}, f32[2,2048,...) custom-call(f32[16,128]{1,0:T(8,128)} %get-tuple-element.75.sc_ref, ...), custom_call_target="tpu_custom_call" | custom-call | tf_op jit(solution)/shard_map/stage_two_next/pallas_call | solution.py:361

commit v3 on v2

--- a/solution.py
+++ b/solution.py
@@ -441,227 +441,243 @@
     )(grad_pool, res_in, res_mid, merged, up_b, down_b, merge_b)
 
 
-def stage_one_back(grad_in, x, mid, up_b, down_b):
-    def kernel(g_ref, x_ref, mid_ref, u_ref, v_ref, du_ref, dv_ref, du_s, dv_s, x_s, vh_s):
-        tile_id = pl.program_id(0)
-
-        @pl.when(tile_id == 0)
-        def _():
-            du_s[...] = jnp.zeros_like(du_s)
-            dv_s[...] = jnp.zeros_like(dv_s)
-            vh_s[...] = halve(v_ref[...].astype(F32))
-
-        for quarter, start in enumerate(token_parts(x_ref, x_s)):
-            cols = slice(quarter * W1, (quarter + 1) * W1)
-            grad = g_ref[:, cols]
+AXIS_STEP = (2, 8, 32)
+MAIN_UNITS = (13, 13, 13, 13, 12, 12)
+LATE_UNITS = (2, 2)
+MAIN = tuple(range(len(MAIN_UNITS)))
+LATE = tuple(range(len(MAIN_UNITS), len(MAIN_UNITS) + len(LATE_UNITS)))
+MAIN_HALF = UNIT * sum(MAIN_UNITS)
+LATE_HALF = UNIT * sum(LATE_UNITS)
+TOTAL = 2 * (MAIN_HALF + LATE_HALF)
+COUNTS = (512,) * 4 + (128, 256) + (32,) * 4
+SEGMENTS = (1024, 1024, 128, 256)
+LOOPS = ((0, 2), (2, 6), (6, 8))
+HOPS = 6
+
+
+def stream_plan():
+    plan, base, slot = [], 0, 0
+    for index, units in enumerate(MAIN_UNITS + LATE_UNITS):
+        hops = [((index // 2 + turn // 2) % 3, (index + turn) % 2) for turn in range(HOPS)]
+        plan.append((units, base, slot, hops))
+        base += UNIT * units
+        slot += (UNIT + 1) * units
+    return plan, slot
+
+
+def sum_grads(parts, acts, squares):
+    plan, slot_units = stream_plan()
+    count = len(plan)
+
+    def kernel(*refs):
+        refs = list(refs)
+        take = lambda number: [refs.pop(0) for _ in range(number)]
+        part_refs, sq_refs = take(len(parts)), take(len(squares))
+        g_ref, x_ref, mid_ref, u_ref, v_ref, out_ref, scale_ref = take(7)
+        flat, pair_buf, slots, x_s, vh_s, du_s, dv_s, load_sem, out_sem, pair_send, pair_recv, back_send, back_recv, hop_send, hop_recv, ready = refs
+        me = lax.axis_index('data')
+        core = lax.rem(me, 2)
+        peer = me + 1 - 2 * core
+        partner, bit = {}, {}
+        for axis, step in enumerate(AXIS_STEP):
+            spot = lax.rem(me // step, 4)
+            partner[axis, 0] = me + (1 - 2 * lax.rem(spot, 2)) * step
+            partner[axis, 1] = me + (3 - 2 * spot) * step
+            bit[axis, 0] = lax.rem((spot + 1) // 2, 2)
+            bit[axis, 1] = spot // 2
+
+        loads = [pltpu.make_async_copy(part_refs[k], flat.at[pl.ds(sum(SEGMENTS[:k]), size)], load_sem.at[k]) for k, size in enumerate(SEGMENTS)]
+        for load in loads:
+            load.start()
+        barrier = pltpu.get_barrier_semaphore()
+        for other in [peer] + list(partner.values()):
+            pl.semaphore_signal(barrier, inc=1, device_id=(other,), device_id_type=pl.DeviceIdType.MESH)
+        x_s[...] = x_ref[...].astype(F32)
+        vh_s[...] = halve(v_ref[...].astype(F32))
+        du_s[...] = jnp.zeros_like(du_s)
+        dv_s[...] = jnp.zeros_like(dv_s)
+        pl.semaphore_wait(barrier, 1 + len(partner))
+        for load in loads:
+            load.wait()
+
+        def send(src, dst, send_sem, recv_sem, device):
+            copy = pltpu.make_async_remote_copy(src_ref=src, dst_ref=dst, send_sem=send_sem, recv_sem=recv_sem, device_id=(device,), device_id_type=pl.DeviceIdType.MESH)
+            copy.start()
+            return copy
+
+        def add_in(start, src, src_start, units, blocks):
+            def body(index, carry):
+                at = pl.ds(start + index * units, units)
+                flat[at] = flat[at] + src[pl.ds(src_start + index * units, units)]
+                return carry
+            lax.fori_loop(0, blocks, body, 0)
+
+        def home(k, side):
+            return plan[k][1] + (MAIN_HALF + side * LATE_HALF if k in LATE else side * MAIN_HALF)
+
+        kept, gone = [[] for _ in plan], [[] for _ in plan]
+        for k, (units, base, slot, hops) in enumerate(plan):
+            start = home(k, core)
+            for turn in range(4):
+                size = (8 >> turn) * units
+                flag = bit[hops[turn]]
+                gone[k].append(start + (1 - flag) * size)
+                start = start + flag * size
+                kept[k].append(start)
+        copies, pairs, backs, outs = {}, {}, {}, []
+
+        def pair_up(streams):
+            for k in streams:
+                size = UNIT * plan[k][0]
+                pairs[k] = send(flat.at[pl.ds(home(k, 1 - core), size)], pair_buf.at[pl.ds(plan[k][1], size)], pair_send.at[k], pair_recv.at[k], peer)
+
+        def slot_at(k, turn):
+            units, slot = plan[k][0], plan[k][2]
+            return slot + sum((8 >> t) if t < 4 else 1 for t in range(turn)) * units
+
+        def hop(k, turn):
+            units, hops = plan[k][0], plan[k][3]
+            size = (8 >> turn) * units if turn < 4 else units
+            src = gone[k][turn] if turn < 4 else kept[k][3]
+            copies[k, turn] = send(flat.at[pl.ds(src, size)], slots.at[pl.ds(slot_at(k, turn), size)], hop_send.at[k, turn], hop_recv.at[k, turn], partner[hops[turn]])
+
+        def first_hops(streams):
+            for k in streams:
+                units, base = plan[k][:2]
+                pairs[k].wait_recv()
+                add_in(gone[k][0], pair_buf, base + gone[k][0] - home(k, core), units, 8)
+                hop(k, 0)
+                add_in(kept[k][0], pair_buf, base + kept[k][0] - home(k, core), units, 8)
+
+        def tell(k, turn, device):
+            pl.semaphore_signal(ready.at[k, turn], inc=1, device_id=(device,), device_id_type=pl.DeviceIdType.MESH)
+
+        def reduce_turn(streams, turn):
+            if turn == HOPS - 1:
+                for k in streams:
+                    pairs[k].wait_send()
+                    tell(k, 4, peer)
+                    for early in range(4):
+                        copies[k, early].wait_send()
+                        tell(k, early, partner[plan[k][3][early]])
+            for k in streams:
+                units = plan[k][0]
+                copies[k, turn].wait_recv()
+                if turn < 3:
+                    blocks = 4 >> turn
+                    at = slot_at(k, turn) - kept[k][turn]
+                    away, stay = gone[k][turn + 1], kept[k][turn + 1]
+                    add_in(away, slots, at + away, units, blocks)
+                    hop(k, turn + 1)
+                    add_in(stay, slots, at + stay, units, blocks)
+                else:
+                    if turn > 3:
+                        copies[k, turn].wait_send()
+                    add_in(kept[k][3], slots, slot_at(k, turn), units, 1)
+                    if turn < HOPS - 1:
+                        hop(k, turn + 1)
+                    else:
+                        share(k, 3)
+
+        def share(k, turn):
+            region = pl.ds(kept[k][turn], (8 >> turn) * plan[k][0])
+            pl.semaphore_wait(ready.at[k, turn], 1)
+            at = 2 * HOPS - 3 - turn
+            copies[k, at] = send(flat.at[region], flat.at[region], hop_send.at[k, at], hop_recv.at[k, at], partner[plan[k][3][turn]])
+
+        def put(region, index):
+            copy = pltpu.make_async_copy(flat.at[region], out_ref.at[region], out_sem.at[index])
+            copy.start()
+            outs.append(copy)
+
+        def gather_turn(streams, turn):
+            for k in streams:
+                copies[k, 2 * HOPS - 3 - turn].wait_recv()
+                if turn:
+                    share(k, turn - 1)
+                if turn < 2:
+                    region = pl.ds(kept[k][0] if turn else gone[k][0], 8 * plan[k][0])
+                    if turn:
+                        pl.semaphore_wait(ready.at[k, 4], 1)
+                    backs[k, turn] = send(flat.at[region], flat.at[region], back_send.at[k, turn], back_recv.at[k, turn], peer)
+                    put(region, 3 * k + turn)
+
+        def token_block(index, carry):
+            quarter, tile = lax.rem(index, 4), index // 4
+            rows = pl.ds(pl.multiple_of(tile * TILE, UNIT), TILE)
+            cols = pl.ds(pl.multiple_of(quarter * W1, W1), W1)
+            grad = g_ref[rows, cols]
             for layer in (1, 0):
-                normed, inv = ln_parts(mid_ref[:, cols].astype(F32) if layer else start)
+                source = mid_ref[rows, cols].astype(F32) if layer else x_s[pl.ds(tile * TOKENS + quarter, TILE, stride=4), :]
+                normed, inv = ln_parts(source)
                 normed_b = normed.astype(BF16)
                 act, slope = gelu_both(dot_nn(normed_b, u_ref[layer]))
                 grad_pre = (dot_nt(grad, vh_s[layer]) * slope).astype(BF16)
                 du_s[layer] += dot_tn(normed_b, grad_pre)
                 dv_s[layer] += dot_tn(grad, act.astype(BF16))
                 if layer:
-                    grad_norm = dot_nt(grad_pre, u_ref[layer])
-                    grad = (ln_back(normed, inv + inv, grad_norm) + grad.astype(F32)).astype(BF16)
-
-        @pl.when(tile_id == NT - 1)
-        def _():
-            for layer in range(2):
-                put_units(du_ref, 32 * layer, du_s[layer].astype(BF16))
-                put_units(dv_ref, 32 * layer, dv_s[layer].T.astype(BF16))
-
-    tile = rows_spec(TILE, W2)
-    return pl.pallas_call(
-        kernel,
-        grid=(NT,),
-        in_specs=[tile, rows_spec(TOKENS, W1), tile] + [whole(s) for s in ONE_SHAPES[:2]],
-        out_specs=[whole((64, UNIT, LANES))] * 2,
-        out_shape=[unit_struct(64)] * 2,
-        scratch_shapes=[pltpu.VMEM(ONE_SHAPES[0], F32), pltpu.VMEM(ONE_SHAPES[0], F32), pltpu.VMEM((TOKENS, W1), F32), pltpu.VMEM(ONE_SHAPES[1], BF16)],
-        compiler_params=params(),
-        name="stage_one_back",
-    )(grad_in, x, mid, up_b, down_b)
-
-
-AXIS_STEP = (2, 8, 32)
-STREAM_UNITS = (14, 14, 13, 13, 13, 13)
-HALF = 1280
-TOTAL = 2 * HALF
-COUNTS = (512,) * 4 + (128, 256) + (32,) * 4
-SEGMENTS = (1024, 1024, 128, 256, 64, 64)
-
-
-def stream_plan():
-    plan, base, slot = [], 0, 0
-    for index, units in enumerate(STREAM_UNITS):
-        order, sub = index // 2, index % 2
-        axes = [(order + shift) % 3 for shift in range(3)]
-        hops = [(axis, (sub + turn) % 2) for axis in axes for turn in range(2)]
-        plan.append((units, base, slot, hops))
-        base += 16 * units
-        slot += 17 * units
-    return plan, slot
-
-
-def sum_grads(parts, squares):
-    plan, slot_units = stream_plan()
-    count = len(plan)
-
-    def kernel(*refs):
-        part_refs, sq_refs = refs[:6], refs[6:12]
-        out_ref, scale_ref, flat, pair_buf, slots, load_sem, out_sem, pair_send, pair_recv, back_send, back_recv, hop_send, hop_recv, ready = refs[12:]
-        me = lax.axis_index('data')
-        core = lax.rem(me, 2)
-        peer = me + 1 - 2 * core
-        mine = core * HALF
-        theirs = (1 - core) * HALF
-        spots = [lax.rem(me // step, 4) for step in AXIS_STEP]
-        partner, bit = {}, {}
-        for axis in range(3):
-            spot = spots[axis]
-            partner[axis, 0] = me + (1 - 2 * lax.rem(spot, 2)) * AXIS_STEP[axis]
-            partner[axis, 1] = me + (3 - 2 * spot) * AXIS_STEP[axis]
-            bit[axis, 0] = lax.rem((spot + 1) // 2, 2)
-            bit[axis, 1] = spot // 2
-
-        loads = [pltpu.make_async_copy(part_refs[k], flat.at[pl.ds(sum(SEGMENTS[:k]), size)], load_sem.at[k]) for k, size in enumerate(SEGMENTS)]
-        for load in loads:
-            load.start()
-        barrier = pltpu.get_barrier_semaphore()
-        for other in [peer] + list(partner.values()):
-            pl.semaphore_signal(barrier, inc=1, device_id=(other,), device_id_type=pl.DeviceIdType.MESH)
-        pl.semaphore_wait(barrier, 7)
-        for load in loads:
-            load.wait()
-
-        def send(src, dst, send_sem, recv_sem, device):
-            copy = pltpu.make_async_remote_copy(src_ref=src, dst_ref=dst, send_sem=send_sem, recv_sem=recv_sem, device_id=(device,), device_id_type=pl.DeviceIdType.MESH)
-            copy.start()
-            return copy
-
-        def add_in(start, src, src_start, units, blocks):
-            def body(index, carry):
-                at = pl.ds(start + index * units, units)
-                flat[at] = flat[at] + src[pl.ds(src_start + index * units, units)]
-                return carry
-            lax.fori_loop(0, blocks, body, 0)
-
-        pairs = [send(flat.at[pl.ds(theirs + base, 16 * units)], pair_buf.at[pl.ds(base, 16 * units)], pair_send.at[k], pair_recv.at[k], peer) for k, (units, base, slot, hops) in enumerate(plan)]
-        held = [mine + base for units, base, slot, hops in plan]
-        kept, gone = [[] for _ in plan], [[] for _ in plan]
-        for k, (units, base, slot, hops) in enumerate(plan):
-            start = held[k]
-            for turn in range(4):
-                size = (8 >> turn) * units
-                flag = bit[hops[turn]]
-                gone[k].append(start + (1 - flag) * size)
-                start = start + flag * size
-                kept[k].append(start)
-        copies = {}
-
-        def slot_at(k, turn):
-            units, slot = plan[k][0], plan[k][2]
-            return slot + sum((8 >> t) if t < 4 else 1 for t in range(turn)) * units
-
-        def hop(k, turn):
-            units, hops = plan[k][0], plan[k][3]
-            size = (8 >> turn) * units if turn < 4 else units
-            src = gone[k][turn] if turn < 4 else kept[k][3]
-            copies[k, turn] = send(flat.at[pl.ds(src, size)], slots.at[pl.ds(slot_at(k, turn), size)], hop_send.at[k, turn], hop_recv.at[k, turn], partner[hops[turn]])
-
-        for k in range(count):
-            units, base = plan[k][:2]
-            pairs[k].wait_recv()
-            add_in(gone[k][0], pair_buf, gone[k][0] - mine, units, 8)
-            hop(k, 0)
-            add_in(kept[k][0], pair_buf, kept[k][0] - mine, units, 8)
-        def tell(k, turn, device):
-            pl.semaphore_signal(ready.at[k, turn], inc=1, device_id=(device,), device_id_type=pl.DeviceIdType.MESH)
-
-        for turn in range(6):
-            if turn == 5:
-                for k in range(count):
-                    pairs[k].wait_send()
-                    tell(k, 4, peer)
-                    for early in range(4):
-                        copies[k, early].wait_send()
-                        tell(k, early, partner[plan[k][3][early]])
-            for k in range(count):
-                units = plan[k][0]
-                copies[k, turn].wait_recv()
-                if turn < 3:
-                    blocks = 4 >> turn
-                    for dst in (gone[k][turn + 1], kept[k][turn + 1]):
-                        add_in(dst, slots, slot_at(k, turn) + dst - kept[k][turn], units, blocks)
-                        if dst is gone[k][turn + 1]:
-                            hop(k, turn + 1)
-                else:
-                    if turn > 3:
-                        copies[k, turn].wait_send()
-                    add_in(kept[k][3], slots, slot_at(k, turn), units, 1)
-                    if turn < 5:
-                        hop(k, turn + 1)
-        outs = []
-
-        def share(k, turn):
-            units, hops = plan[k][0], plan[k][3]
-            region = pl.ds(kept[k][turn], (8 >> turn) * units)
-            pl.semaphore_wait(ready.at[k, turn], 1)
-            copies[k, 9 - turn] = send(flat.at[region], flat.at[region], hop_send.at[k, 9 - turn], hop_recv.at[k, 9 - turn], partner[hops[turn]])
-
-        def put(region, index):
-            copy = pltpu.make_async_copy(flat.at[region], out_ref.at[region], out_sem.at[index])
-            copy.start()
-            outs.append(copy)
-
-        backs = {}
-        for k in range(count):
-            share(k, 3)
+                    grad = (ln_back(normed, inv + inv, dot_nt(grad_pre, u_ref[layer])) + grad.astype(F32)).astype(BF16)
+            return carry
+
+        pair_up(MAIN)
+        for number, (low, high) in enumerate(LOOPS):
+            lax.fori_loop(low, high, token_block, 0)
+            if number == 0:
+                first_hops(MAIN)
+            elif number == 1:
+                reduce_turn(MAIN, 0)
+        for layer in range(2):
+            late = sum(SEGMENTS) + layer * (LATE_HALF // 2)
+            put_units(flat, late, du_s[layer].astype(BF16))
+            put_units(flat, late + LATE_HALF, dv_s[layer].T.astype(BF16))
+        pair_up(LATE)
+        reduce_turn(MAIN, 1)
+        first_hops(LATE)
+        for turn in range(2, HOPS):
+            reduce_turn(MAIN, turn)
+            reduce_turn(LATE, turn - 2)
+        gather_turn(MAIN, 3)
+        reduce_turn(LATE, HOPS - 2)
+        gather_turn(MAIN, 2)
+        reduce_turn(LATE, HOPS - 1)
+        gather_turn(MAIN, 1)
         for turn in (3, 2, 1, 0):
-            for k in range(count):
-                units = plan[k][0]
-                copies[k, 9 - turn].wait_recv()
-                if turn:
-                    share(k, turn - 1)
-                if turn < 2:
-                    region = pl.ds(kept[k][0] if turn else gone[k][0], 8 * units)
-                    if turn:
-                        pl.semaphore_wait(ready.at[k, 4], 1)
-                    backs[k, turn] = send(flat.at[region], flat.at[region], back_send.at[k, turn], back_recv.at[k, turn], peer)
-                    put(region, 4 * k + turn)
+            gather_turn(LATE, turn)
+        gather_turn(MAIN, 0)
         for k in range(count):
             for turn in (1, 0):
                 backs[k, turn].wait_recv()
-            put(pl.ds(theirs + plan[k][1], 16 * plan[k][0]), 4 * k + 2)
-        squares = [ref.at[row] for ref in sq_refs for row in range(ref.shape[0])]
+            put(pl.ds(home(k, 1 - core), UNIT * plan[k][0]), 3 * k + 2)
+        squares_list = [ref.at[row] for ref in sq_refs for row in range(ref.shape[0])]
         for index, size in enumerate(COUNTS):
             def body(step, total, first=sum(COUNTS[:index])):
                 block = flat[pl.ds(first + step * UNIT, UNIT)].astype(F32)
                 return total + jnp.sum(block * block, axis=HERE_AXES, keepdims=True)[0]
             grad_sq = jnp.sum(lax.fori_loop(0, size // UNIT, body, jnp.zeros((1, LANES), F32)), axis=-1, keepdims=True)
-            weight_sq = jnp.sum(jnp.sum(squares[index][...], axis=0, keepdims=True), axis=-1, keepdims=True)
+            weight_sq = jnp.sum(jnp.sum(squares_list[index][...], axis=0, keepdims=True), axis=-1, keepdims=True)
             scale_ref[pl.ds(index, 1), :] = jnp.broadcast_to(TRUST * (jnp.sqrt(weight_sq) / jnp.sqrt(grad_sq)), (1, LANES))
         for copy in outs:
             copy.wait()
         for k in range(count):
             for turn in (1, 0):
                 backs[k, turn].wait_send()
-            for turn in range(6, 10):
-                copies[k, turn].wait_send()
+            for turn in range(4):
+                copies[k, HOPS + turn].wait_send()
 
     anywhere = pl.BlockSpec(memory_space=pl.ANY)
     vmem = pl.BlockSpec(memory_space=pltpu.VMEM)
     dma = pltpu.SemaphoreType.DMA
+    units = lambda number: pltpu.VMEM((number, UNIT, LANES), BF16)
+    both, each = (count, 2), (count, HOPS + 4)
     return pl.pallas_call(
         kernel,
-        in_specs=[anywhere] * 6 + [vmem] * 6,
+        in_specs=[anywhere] * len(parts) + [vmem] * (len(squares) + len(acts)),
         out_specs=[anywhere, vmem],
         out_shape=[unit_struct(TOTAL), struct(SCALE_SHAPE, F32)],
-        scratch_shapes=[pltpu.VMEM((TOTAL, UNIT, LANES), BF16), pltpu.VMEM((HALF, UNIT, LANES), BF16), pltpu.VMEM((slot_units, UNIT, LANES), BF16), dma((6,)), dma((4 * count,)), dma((count,)), dma((count,)), dma((count, 2)), dma((count, 2)), dma((count, 10)), dma((count, 10)), pltpu.SemaphoreType.REGULAR((count, 5))],
+        scratch_shapes=[units(TOTAL), units(MAIN_HALF + LATE_HALF), units(slot_units), pltpu.VMEM((4 * ROWS, W1), F32), pltpu.VMEM(ONE_SHAPES[1], BF16), pltpu.VMEM(ONE_SHAPES[0], F32), pltpu.VMEM(ONE_SHAPES[0], F32), dma((len(parts),)), dma((3 * count,)), dma((count,)), dma((count,)), dma(both), dma(both), dma(each), dma(each), pltpu.SemaphoreType.REGULAR((count, 5))],
         compiler_params=params(collective_id=0, has_side_effects=True),
         name="sum_grads",
-    )(*parts, *squares)
+    )(*parts, *squares, *acts)
 
 
 def solution(mesh):
@@ -674,8 +690,7 @@
         mid, merged, res0, ub1, vb1, mb, su1, sv1, sm = stage_one_now(xn, up_one, down_one, merge_proj)
         res1, ub2, vb2, su2, sv2, sh, dh, grad_pool = stage_two_now(res0, labels_now, up_two, down_two, head_proj.T, images * data_devs)
         du2, dv2, dm, grad_mid = stage_two_back(grad_pool, res0, res1, merged, ub2, vb2, mb)
-        du1, dv1 = stage_one_back(grad_mid, xn, mid, ub1, vb1)
-        grads, scales = sum_grads((du2, dv2, dm, dh, du1, dv1), (su2, sv2, sm[None], sh[None], su1, sv1))
+        grads, scales = sum_grads((du2, dv2, dm, dh), (grad_mid, xn, mid, ub1, vb1), (su2, sv2, sm[None], sh[None], su1, sv1))
         res_f, nu1, nv1, nm, qu1, qv1, qm = stage_one_next(xf, scales, grads, (up_one, down_one, merge_proj), (vel_up_one, vel_down_one, vel_merge_proj))
         nu2, nv2, nh, qu2, qv2, qh, logits = stage_two_next(res_f, scales, grads, (up_two, down_two, head_proj.T), (vel_up_two, vel_down_two, vel_head_proj.T), images)
         return logits, nu1, nv1, nm, nu2, nv2, nh.T, qu1, qv1, qm, qu2, qv2, qh.T

time: 280 us -> 266 us (0.950)
  Pallas kernels: 273 us -> 259 us
    pallas_call x2 -> x1, Pallas kernels: 119 us -> 105 us  [sum_grads(): pl.pallas_call(kernel, in_specs=[anywhere] * len(parts) + [vmem] * (len(s...]
where the time goes in v3:
time: 266 us; the launch traced here: 262 us
  Pallas kernels  259 us (97%)
    pallas_call x1, Pallas kernels, sum_grads(): pl.pallas_call(kernel, in_specs=[anywhere] * len(parts) + [vmem] * (len(s...  105 us
    pallas_call x1, Pallas kernels, stage_two_back(): pl.pallas_call(kernel, grid=(2, NCH), in_specs=[whole((128, W2)), act, ac...  57.8 us
    pallas_call x1, Pallas kernels, stage_two_next(): pl.pallas_call(kernel, grid=(2, NF), in_specs=[whole(SCALE_SHAPE), whole(...  35 us
    pallas_call x1, Pallas kernels, stage_two_now(): pl.pallas_call(kernel, grid=(2, NF), in_specs=[whole((ROWS, W2)), whole((...  26.5 us
    pallas_call x1, Pallas kernels, stage_one_next(): pl.pallas_call(kernel, grid=(NT,), in_specs=[whole(SCALE_SHAPE), rows_spe...  18 us
    pallas_call x1, Pallas kernels, stage_one_now(): pl.pallas_call(kernel, grid=(NT,), in_specs=[rows_spec(TOKENS, W1)] + [wh...  16.9 us

profile of v3, /device:TPU:1, one launch (start us, length us, event | category | flops | bytes accessed | tf_op | source)
XLA Modules:
  0.0 261.5 jit_solution(13387391367349172507)
XLA Ops:
  0.6 0.7 pad_bitcast_fusion
  1.3 0.7 copy.28.lab_ref
  2.0 16.9 %stage_one_now.1 = (bf16[1568,512]{1,0:T(8,128)(2,1)}, bf16[1568,512]{1,0:T(8,128)(2,1)}, bf16[1568,512]{1,0:T(8,128)(2,1)}, bf16[2,128,512]{2,1,0:T(8,128)(2,1)...) custom-call(bf16[6272,128]{1,0:T(8,128)(2,1)} %bitcast.12, ...), custom_call_target="tpu_custom_call" | custom-call | tf_op jit(solution)/shard_map/stage_one_now/pallas_call | solution.py:170
  18.9 26.5 %stage_two_now.1 = (bf16[1568,512]{1,0:T(8,128)(2,1)}, bf16[2,512,2048]{2,1,0:T(8,128)(2,1)}, bf16[2,2048,512]{2,1,0:T(8,128)(2,1)}, f32[2,8,1024]{2,1,0:T(8,128...) custom-call(bf16[1568,512]{1,0:T(8,128)(2,1)} %get-tuple-element.50.r_ref, ...), custom_call_target="tpu_custom_call" | custom-call | tf_op jit(solution)/shard_map/stage_two_now/pallas_call | solution.py:311
  45.4 57.8 %stage_two_back.1 = (bf16[1024,16,128]{2,1,0:T(8,128)(2,1)}, bf16[1024,16,128]{2,1,0:T(8,128)(2,1)}, bf16[128,16,128]{2,1,0:T(8,128)(2,1)}, bf16[1568,512]{1,0:T(8,128)(2,1)}) custom-call(bf16[128,512]{1,0:T(8,128)(2,1)} %get-tuple-element.51.gp_ref, bf16[1568,512]{1,0:T(8,128)(2,1)} %get-tuple-element.50.r_ref.r0_ref, ...), custom_call_target="tpu_custom_call" | custom-call | tf_op jit(solution)/shard_map/stage_two_back/pallas_call | solution.py:432
  103.2 105.1 %sum_grads.1 = (bf16[2560,16,128]{2,1,0:T(8,128)(2,1)}, f32[16,128]{1,0:T(8,128)}) custom-call(bf16[1024,16,128]{2,1,0:T(8,128)(2,1)} %get-tuple-element.57.refs_0_, bf16[1024,16,128]{2,1,0:T(8,128)(2,1)} %get-tuple-element.58.refs_1_, bf16[128,16,128]{2,1,0:T(8,128)(2,1)} %get-tuple-element.59.refs_2_, bf16[256,16,128]{2,1,0:T(8,128)(2,1)} %get-tuple-element.60.refs_3_, ...), custom_call_target="tpu_custom_call" | custom-call | tf_op jit(solution)/shard_map/sum_grads/pallas_call | solution.py:672
  208.3 18.0 %stage_one_next.1 = (bf16[1568,512]{1,0:T(8,128)(2,1)}, f32[2,128,512]{2,1,0:T(8,128)}, f32[2,512,128]{2,1,0:T(8,128)}, f32[512,512]{1,0:T(8,128)}, f32[2,128,51...) custom-call(f32[16,128]{1,0:T(8,128)} %get-tuple-element.71.sc_ref, bf16[6272,128]{1,0:T(8,128)(2,1)} %bitcast.15, ...), custom_call_target="tpu_custom_call" | custom-call | tf_op jit(solution)/shard_map/stage_one_next/pallas_call | solution.py:198
  226.3 35.0 %stage_two_next.1 = (f32[2,512,2048]{2,1,0:T(8,128)}, f32[2,2048,512]{2,1,0:T(8,128)}, f32[1000,512]{1,0:T(8,128)}, f32[2,512,2048]{2,1,0:T(8,128)}, f32[2,2048,...) custom-call(f32[16,128]{1,0:T(8,128)} %get-tuple-element.71.sc_ref, ...), custom_call_target="tpu_custom_call" | custom-call | tf_op jit(solution)/shard_map/stage_two_next/pallas_call | solution.py:361

commit v4 on v3

--- a/solution.py
+++ b/solution.py
@@ -56,18 +56,31 @@
     return lax.dot_general(lhs, rhs, (((0,), (0,)), ((), ())), preferred_element_type=F32)
 
 
+def row_mean(values):
+    return jnp.mean(values, axis=-1, keepdims=True)
+
+
+def row_sum(values):
+    return jnp.sum(values, axis=-1, keepdims=True)
+
+
+def scale_of(ref, index):
+    return ref[pl.ds(index, 1), :1]
+
+
 def ln_parts(values):
-    row_mean = jnp.mean(values, axis=-1, keepdims=True)
-    centered = values - row_mean
-    variance = jnp.mean(centered * centered, axis=-1, keepdims=True)
+    centered = values - row_mean(values)
+    variance = row_mean(centered * centered)
     inv = lax.rsqrt(variance + LN_EPS)
     return centered * inv, inv
 
 
 def ln_back(normed, inv, grad):
-    mean_grad = jnp.mean(grad, axis=-1, keepdims=True)
-    mean_dot = jnp.mean(grad * normed, axis=-1, keepdims=True)
-    return inv * (grad - mean_grad - normed * mean_dot)
+    return inv * (grad - row_mean(grad) - normed * row_mean(grad * normed))
+
+
+def normalize(values):
+    return ln_parts(values)[0].astype(BF16)
 
 
 def gelu_fwd(half):
@@ -134,7 +147,7 @@
     outs0, outs1 = [], []
     for resid in parts:
         for layer in range(2):
-            normed = ln_parts(resid.astype(F32))[0].astype(BF16)
+            normed = normalize(resid.astype(F32))
             act = gelu_fwd(dot_nn(normed, ub[layer])).astype(BF16)
             resid = (resid.astype(F32) + dot_nn(act, vb[layer])).astype(BF16)
             (outs0, outs1)[layer].append(resid)
@@ -184,9 +197,9 @@
         @pl.when(pl.program_id(0) == 0)
         def _():
             for layer in range(2):
-                nu_ref[layer], qu_ref[layer] = lars_block(u_ref[layer], pu_ref[layer], get_units(gu_ref, 32 * layer, W1, H1), sc_ref[6 + layer:7 + layer, :1])
-                nv_ref[layer], qv_ref[layer] = lars_block(v_ref[layer], pv_ref[layer], get_units(gv_ref, 32 * layer, H1, W1), sc_ref[8 + layer:9 + layer, :1])
-            nm_ref[...], qm_ref[...] = lars_block(m_ref[...], pm_ref[...], get_units(gm_ref, 0, W2, W2), sc_ref[4:5, :1])
+                nu_ref[layer], qu_ref[layer] = lars_block(u_ref[layer], pu_ref[layer], get_units(gu_ref, 32 * layer, W1, H1), scale_of(sc_ref, 6 + layer))
+                nv_ref[layer], qv_ref[layer] = lars_block(v_ref[layer], pv_ref[layer], get_units(gv_ref, 32 * layer, H1, W1), scale_of(sc_ref, 8 + layer))
+            nm_ref[...], qm_ref[...] = lars_block(m_ref[...], pm_ref[...], get_units(gm_ref, 0, W2, W2), scale_of(sc_ref, 4))
             ub_ref[...] = halve(nu_ref[...])
             vb_ref[...] = nv_ref[...].astype(BF16)
             mb_ref[...] = nm_ref[...].astype(BF16)
@@ -214,7 +227,7 @@
 def stage_two_start(chunk, src_ref, dst_norm, acc_ref):
     for start, size in row_parts():
         resid = src_ref[start:start + size].astype(F32)
-        dst_norm[start:start + size] = ln_parts(resid)[0].astype(BF16)
+        dst_norm[start:start + size] = normalize(resid)
         acc_ref[start:start + size] = resid
 
 
@@ -225,8 +238,8 @@
 
 
 def pool_images(resid_ref):
-    cols = lax.broadcasted_iota(jnp.int32, (16, ROWS_PAD), 1)
-    base = lax.broadcasted_iota(jnp.int32, (16, ROWS_PAD), 0) * PER_IMAGE
+    cols = lax.broadcasted_iota(jnp.int32, (UNIT, ROWS_PAD), 1)
+    base = lax.broadcasted_iota(jnp.int32, (UNIT, ROWS_PAD), 0) * PER_IMAGE
     mask = ((cols >= base) & (cols < base + PER_IMAGE) & (cols < ROWS)).astype(F32).astype(BF16)
     return dot_nn(mask, resid_ref[...]) * (1.0 / PER_IMAGE)
 
@@ -297,27 +310,30 @@
             live = cols < classes
             top = jnp.max(jnp.where(live, logits, -jnp.inf), axis=-1, keepdims=True)
             expd = jnp.where(live, jnp.exp(logits - top), 0.0)
-            probs = expd / jnp.sum(expd, axis=-1, keepdims=True)
-            onehot = (cols == lab_ref[...]).astype(F32)
+            probs = expd / row_sum(expd)
+            target = jnp.zeros_like(cols)
+            for image in range(images):
+                target = jnp.where(rows == image, lab_ref[image], target)
+            onehot = (cols == target).astype(F32)
             grad_logits = jnp.where(rows < images, (probs - onehot) / global_batch, 0.0).astype(BF16)
             grad_head = dot_tn(grad_logits, head_in).astype(BF16)
             for block in range(2 * NF):
                 put_units(dh_ref, block * HEAD_UNITS, grad_head[block * HEAD_ROWS:(block + 1) * HEAD_ROWS])
             grad_pool = ln_back(normed, inv, dot_nn(grad_logits, hb_s[...])) / PER_IMAGE
             gp_ref[...] = jnp.zeros_like(gp_ref)
-            gp_ref[:16] = grad_pool.astype(BF16)
+            gp_ref[:UNIT] = grad_pool.astype(BF16)
 
     u_spec, v_spec, h_spec = two_specs()
     return pl.pallas_call(
         kernel,
         grid=(2, NF),
-        in_specs=[whole((ROWS, W2)), whole((16, 1)), u_spec, v_spec, h_spec],
+        in_specs=[whole((ROWS, W2)), pl.BlockSpec(memory_space=pltpu.SMEM), u_spec, v_spec, h_spec],
         out_specs=[whole((ROWS, W2)), u_spec, v_spec, pl.BlockSpec((1, 8, FCHUNK), by_layer), pl.BlockSpec((1, 8, W2), by_layer), whole((8, W2)), whole((256, UNIT, LANES)), whole((LANES, W2))],
         out_shape=[struct((ROWS, W2), BF16), struct(UP_SHAPE, BF16), struct(DOWN_SHAPE, BF16), struct((2, 8, FCHUNK), F32), struct((2, 8, W2), F32), struct((8, W2), F32), unit_struct(256), struct((LANES, W2), BF16)],
         scratch_shapes=[pltpu.VMEM((ROWS, W2), BF16), pltpu.VMEM((ROWS, W2), F32), pltpu.VMEM((ROWS_PAD, W2), BF16), pltpu.VMEM((HEAD_PAD, W2), BF16)],
         compiler_params=params(),
         name="stage_two_now",
-    )(res_in, jnp.pad(labels, (0, 16 - images))[:, None], up_two, down_two, head)
+    )(res_in, labels, up_two, down_two, head)
 
 
 def stage_two_next(res_in, scales, grads, weights, vels, images):
@@ -336,12 +352,12 @@
             def _():
                 stage_two_start(chunk, res_s, norm_s, acc_s)
 
-        new_u, qu_ref[0] = lars_block(u_ref[0], pu_ref[0], get_units(gu_ref, 0, W2, FCHUNK), sc_ref[pl.ds(layer, 1), :1])
+        new_u, qu_ref[0] = lars_block(u_ref[0], pu_ref[0], get_units(gu_ref, 0, W2, FCHUNK), scale_of(sc_ref, layer))
         nu_ref[0] = new_u
         for part in range(FCHUNK // CHUNK):
             rows = slice(part * CHUNK, (part + 1) * CHUNK)
-            nv_ref[0, rows], qv_ref[0, rows] = lars_block(v_ref[0, rows], pv_ref[0, rows], get_units(gv_ref, part * CHUNK_UNITS, CHUNK, W2), sc_ref[pl.ds(2 + layer, 1), :1])
-        nh_ref[...], qh_ref[...] = lars_block(h_ref[...], ph_ref[...], get_units(gh_ref, 0, HEAD_ROWS, W2), sc_ref[5:6, :1])
+            nv_ref[0, rows], qv_ref[0, rows] = lars_block(v_ref[0, rows], pv_ref[0, rows], get_units(gv_ref, part * CHUNK_UNITS, CHUNK, W2), scale_of(sc_ref, 2 + layer))
+        nh_ref[...], qh_ref[...] = lars_block(h_ref[...], ph_ref[...], get_units(gh_ref, 0, HEAD_ROWS, W2), scale_of(sc_ref, 5))
         at, head_part = head_block(layer, chunk, nh_ref, classes)
         hb_s[pl.ds(at, HEAD_ROWS)] = head_part.astype(BF16)
         stage_two_step(norm_s, acc_s, halve(new_u), nv_ref[0].astype(BF16))
@@ -353,7 +369,7 @@
             @pl.when(layer == 1)
             def _():
                 res_s[ROWS:] = jnp.zeros((ROWS_PAD - ROWS, W2), BF16)
-                head_in = ln_parts(pool_images(res_s))[0].astype(BF16)
+                head_in = normalize(pool_images(res_s))
                 out_ref[...] = dot_nt(head_in, hb_s[...])[:images, :classes]
 
     u_spec, v_spec, h_spec = two_specs()
@@ -387,7 +403,7 @@
             pre_s[ROWS:] = jnp.zeros((ROWS_PAD - ROWS, CHUNK), BF16)
 
         def begin(src_ref):
-            n_s[...] = ln_parts(src_ref[...].astype(F32))[0].astype(BF16)
+            n_s[...] = normalize(src_ref[...].astype(F32))
             nt_s[:, :ROWS] = n_s[...].T
             dn_s[...] = jnp.zeros_like(dn_s)
 
@@ -453,6 +469,8 @@
 SEGMENTS = (1024, 1024, 128, 256)
 LOOPS = ((0, 2), (2, 6), (6, 8))
 HOPS = 6
+PIECES = (0, 1)
+BACKS = (0, 1, 2)
 
 
 def stream_plan():
@@ -491,7 +509,7 @@
             load.start()
         barrier = pltpu.get_barrier_semaphore()
         for other in [peer] + list(partner.values()):
-            pl.semaphore_signal(barrier, inc=1, device_id=(other,), device_id_type=pl.DeviceIdType.MESH)
+            pl.semaphore_signal(barrier, device_id=(other,), device_id_type=pl.DeviceIdType.MESH)
         x_s[...] = x_ref[...].astype(F32)
         vh_s[...] = halve(v_ref[...].astype(F32))
         du_s[...] = jnp.zeros_like(du_s)
@@ -526,81 +544,107 @@
                 kept[k].append(start)
         copies, pairs, backs, outs = {}, {}, {}, []
 
+        def halves(k, start, turn):
+            size = (4 >> turn) * plan[k][0]
+            flag = bit[plan[k][3][turn + 1]]
+            return [(start + (1 - flag) * size, size), (start + flag * size, size)]
+
         def pair_up(streams):
-            for k in streams:
-                size = UNIT * plan[k][0]
-                pairs[k] = send(flat.at[pl.ds(home(k, 1 - core), size)], pair_buf.at[pl.ds(plan[k][1], size)], pair_send.at[k], pair_recv.at[k], peer)
+            for piece, side in enumerate((gone, kept)):
+                for k in streams:
+                    units, base = plan[k][:2]
+                    at = side[k][0] - home(k, core)
+                    pairs[k, piece] = send(flat.at[pl.ds(home(k, 1 - core) + at, 8 * units)], pair_buf.at[pl.ds(base + at, 8 * units)], pair_send.at[k, piece], pair_recv.at[k, piece], peer)
 
         def slot_at(k, turn):
             units, slot = plan[k][0], plan[k][2]
             return slot + sum((8 >> t) if t < 4 else 1 for t in range(turn)) * units
 
+        def pieces_of(k, turn):
+            return halves(k, gone[k][turn], turn) if turn < 3 else [(gone[k][3] if turn < 4 else kept[k][3], plan[k][0])]
+
         def hop(k, turn):
-            units, hops = plan[k][0], plan[k][3]
-            size = (8 >> turn) * units if turn < 4 else units
-            src = gone[k][turn] if turn < 4 else kept[k][3]
-            copies[k, turn] = send(flat.at[pl.ds(src, size)], slots.at[pl.ds(slot_at(k, turn), size)], hop_send.at[k, turn], hop_recv.at[k, turn], partner[hops[turn]])
+            for piece, (src, size) in enumerate(pieces_of(k, turn)):
+                dst = slot_at(k, turn) + (src - gone[k][turn] if turn < 3 else 0)
+                copies[k, turn, piece] = send(flat.at[pl.ds(src, size)], slots.at[pl.ds(dst, size)], hop_send.at[k, turn, piece], hop_recv.at[k, turn, piece], partner[plan[k][3][turn]])
 
         def first_hops(streams):
-            for k in streams:
-                units, base = plan[k][:2]
-                pairs[k].wait_recv()
-                add_in(gone[k][0], pair_buf, base + gone[k][0] - home(k, core), units, 8)
-                hop(k, 0)
-                add_in(kept[k][0], pair_buf, base + kept[k][0] - home(k, core), units, 8)
+            for piece, side in enumerate((gone, kept)):
+                for k in streams:
+                    units, base = plan[k][:2]
+                    pairs[k, piece].wait_recv()
+                    add_in(side[k][0], pair_buf, base + side[k][0] - home(k, core), units, 8)
+                    if piece == 0:
+                        hop(k, 0)
 
         def tell(k, turn, device):
-            pl.semaphore_signal(ready.at[k, turn], inc=1, device_id=(device,), device_id_type=pl.DeviceIdType.MESH)
+            pl.semaphore_signal(ready.at[k, turn], device_id=(device,), device_id_type=pl.DeviceIdType.MESH)
 
         def reduce_turn(streams, turn):
             if turn == HOPS - 1:
                 for k in streams:
-                    pairs[k].wait_send()
+                    for piece in PIECES:
+                        pairs[k, piece].wait_send()
                     tell(k, 4, peer)
                     for early in range(4):
-                        copies[k, early].wait_send()
+                        for piece in range(len(pieces_of(k, early))):
+                            copies[k, early, piece].wait_send()
                         tell(k, early, partner[plan[k][3][early]])
+            if turn < 3:
+                for piece, side in enumerate((gone, kept)):
+                    for k in streams:
+                        copies[k, turn, piece].wait_recv()
+                        dst = side[k][turn + 1]
+                        add_in(dst, slots, slot_at(k, turn) + dst - kept[k][turn], plan[k][0], 4 >> turn)
+                        if piece == 0:
+                            hop(k, turn + 1)
+                return
             for k in streams:
-                units = plan[k][0]
-                copies[k, turn].wait_recv()
-                if turn < 3:
-                    blocks = 4 >> turn
-                    at = slot_at(k, turn) - kept[k][turn]
-                    away, stay = gone[k][turn + 1], kept[k][turn + 1]
-                    add_in(away, slots, at + away, units, blocks)
+                copies[k, turn, 0].wait_recv()
+                if turn > 3:
+                    copies[k, turn, 0].wait_send()
+                add_in(kept[k][3], slots, slot_at(k, turn), plan[k][0], 1)
+                if turn < HOPS - 1:
                     hop(k, turn + 1)
-                    add_in(stay, slots, at + stay, units, blocks)
                 else:
-                    if turn > 3:
-                        copies[k, turn].wait_send()
-                    add_in(kept[k][3], slots, slot_at(k, turn), units, 1)
-                    if turn < HOPS - 1:
-                        hop(k, turn + 1)
-                    else:
-                        share(k, 3)
-
-        def share(k, turn):
-            region = pl.ds(kept[k][turn], (8 >> turn) * plan[k][0])
-            pl.semaphore_wait(ready.at[k, turn], 1)
+                    share(k, 3, 0)
+                    share(k, 2, 0)
+
+        def spread(k, turn):
+            if turn > 2:
+                return [(kept[k][3], plan[k][0])]
+            return halves(k, kept[k][turn], turn)[::-1]
+
+        def share(k, turn, piece):
+            start, size = spread(k, turn)[piece]
+            if piece == 0:
+                pl.semaphore_wait(ready.at[k, turn], 1)
             at = 2 * HOPS - 3 - turn
-            copies[k, at] = send(flat.at[region], flat.at[region], hop_send.at[k, at], hop_recv.at[k, at], partner[plan[k][3][turn]])
+            copies[k, at, piece] = send(flat.at[pl.ds(start, size)], flat.at[pl.ds(start, size)], hop_send.at[k, at, piece], hop_recv.at[k, at, piece], partner[plan[k][3][turn]])
 
         def put(region, index):
             copy = pltpu.make_async_copy(flat.at[region], out_ref.at[region], out_sem.at[index])
             copy.start()
             outs.append(copy)
 
+        def back(k, index, start, size):
+            region = pl.ds(start, size)
+            backs[k, index] = send(flat.at[region], flat.at[region], back_send.at[k, index], back_recv.at[k, index], peer)
+            put(region, 4 * k + index)
+
         def gather_turn(streams, turn):
-            for k in streams:
-                copies[k, 2 * HOPS - 3 - turn].wait_recv()
-                if turn:
-                    share(k, turn - 1)
-                if turn < 2:
-                    region = pl.ds(kept[k][0] if turn else gone[k][0], 8 * plan[k][0])
-                    if turn:
-                        pl.semaphore_wait(ready.at[k, 4], 1)
-                    backs[k, turn] = send(flat.at[region], flat.at[region], back_send.at[k, turn], back_recv.at[k, turn], peer)
-                    put(region, 3 * k + turn)
+            for piece in range(2 if turn < 3 else 1):
+                for k in streams:
+                    copies[k, 2 * HOPS - 3 - turn, piece].wait_recv()
+                    if turn == 0:
+                        back(k, 1 + piece, *halves(k, gone[k][0], 0)[1 - piece])
+                    elif piece or turn > 2:
+                        share(k, turn - 1, 1)
+                        if turn > 1:
+                            share(k, turn - 2, 0)
+                        else:
+                            pl.semaphore_wait(ready.at[k, 4], 1)
+                            back(k, 0, kept[k][0], 8 * plan[k][0])
 
         def token_block(index, carry):
             quarter, tile = lax.rem(index, 4), index // 4
@@ -645,36 +689,37 @@
             gather_turn(LATE, turn)
         gather_turn(MAIN, 0)
         for k in range(count):
-            for turn in (1, 0):
-                backs[k, turn].wait_recv()
-            put(pl.ds(home(k, 1 - core), UNIT * plan[k][0]), 3 * k + 2)
+            for index in BACKS:
+                backs[k, index].wait_recv()
+            put(pl.ds(home(k, 1 - core), UNIT * plan[k][0]), 4 * k + 3)
         squares_list = [ref.at[row] for ref in sq_refs for row in range(ref.shape[0])]
         for index, size in enumerate(COUNTS):
             def body(step, total, first=sum(COUNTS[:index])):
                 block = flat[pl.ds(first + step * UNIT, UNIT)].astype(F32)
                 return total + jnp.sum(block * block, axis=HERE_AXES, keepdims=True)[0]
-            grad_sq = jnp.sum(lax.fori_loop(0, size // UNIT, body, jnp.zeros((1, LANES), F32)), axis=-1, keepdims=True)
-            weight_sq = jnp.sum(jnp.sum(squares_list[index][...], axis=0, keepdims=True), axis=-1, keepdims=True)
+            grad_sq = row_sum(lax.fori_loop(0, size // UNIT, body, jnp.zeros((1, LANES), F32)))
+            weight_sq = row_sum(jnp.sum(squares_list[index][...], axis=0, keepdims=True))
             scale_ref[pl.ds(index, 1), :] = jnp.broadcast_to(TRUST * (jnp.sqrt(weight_sq) / jnp.sqrt(grad_sq)), (1, LANES))
         for copy in outs:
             copy.wait()
         for k in range(count):
-            for turn in (1, 0):
-                backs[k, turn].wait_send()
+            for index in BACKS:
+                backs[k, index].wait_send()
             for turn in range(4):
-                copies[k, HOPS + turn].wait_send()
+                for piece in range(len(spread(k, turn))):
+                    copies[k, 2 * HOPS - 3 - turn, piece].wait_send()
 
     anywhere = pl.BlockSpec(memory_space=pl.ANY)
     vmem = pl.BlockSpec(memory_space=pltpu.VMEM)
     dma = pltpu.SemaphoreType.DMA
     units = lambda number: pltpu.VMEM((number, UNIT, LANES), BF16)
-    both, each = (count, 2), (count, HOPS + 4)
+    both, each = (count, 3), (count, HOPS + 4, 2)
     return pl.pallas_call(
         kernel,
         in_specs=[anywhere] * len(parts) + [vmem] * (len(squares) + len(acts)),
         out_specs=[anywhere, vmem],
         out_shape=[unit_struct(TOTAL), struct(SCALE_SHAPE, F32)],
-        scratch_shapes=[units(TOTAL), units(MAIN_HALF + LATE_HALF), units(slot_units), pltpu.VMEM((4 * ROWS, W1), F32), pltpu.VMEM(ONE_SHAPES[1], BF16), pltpu.VMEM(ONE_SHAPES[0], F32), pltpu.VMEM(ONE_SHAPES[0], F32), dma((len(parts),)), dma((3 * count,)), dma((count,)), dma((count,)), dma(both), dma(both), dma(each), dma(each), pltpu.SemaphoreType.REGULAR((count, 5))],
+        scratch_shapes=[units(TOTAL), units(MAIN_HALF + LATE_HALF), units(slot_units), pltpu.VMEM((4 * ROWS, W1), F32), pltpu.VMEM(ONE_SHAPES[1], BF16), pltpu.VMEM(ONE_SHAPES[0], F32), pltpu.VMEM(ONE_SHAPES[0], F32), dma((len(parts),)), dma((4 * count,)), dma(both), dma(both), dma(both), dma(both), dma(each), dma(each), pltpu.SemaphoreType.REGULAR((count, 5))],
         compiler_params=params(collective_id=0, has_side_effects=True),
         name="sum_grads",
     )(*parts, *squares, *acts)

time: 266 us -> 263 us (0.989)
  no operation moved by 1% of the time
where the time goes in v4:
time: 263 us; the launch traced here: 258 us
  Pallas kernels  257 us (98%)
    pallas_call x1, Pallas kernels, sum_grads(): pl.pallas_call(kernel, in_specs=[anywhere] * len(parts) + [vmem] * (len(s...  103 us
    pallas_call x1, Pallas kernels, stage_two_back(): pl.pallas_call(kernel, grid=(2, NCH), in_specs=[whole((128, W2)), act, ac...  57.8 us
    pallas_call x1, Pallas kernels, stage_two_next(): pl.pallas_call(kernel, grid=(2, NF), in_specs=[whole(SCALE_SHAPE), whole(...  35 us
    pallas_call x1, Pallas kernels, stage_two_now(): pl.pallas_call(kernel, grid=(2, NF), in_specs=[whole((ROWS, W2)), pl.Bloc...  26.5 us
    pallas_call x1, Pallas kernels, stage_one_next(): pl.pallas_call(kernel, grid=(NT,), in_specs=[whole(SCALE_SHAPE), rows_spe...  18 us
    pallas_call x1, Pallas kernels, stage_one_now(): pl.pallas_call(kernel, grid=(NT,), in_specs=[rows_spec(TOKENS, W1)] + [wh...  16.9 us

profile of v4, /device:TPU:1, one launch (start us, length us, event | category | flops | bytes accessed | tf_op | source)
XLA Modules:
  0.0 258.1 jit_solution(121126921373916143)
XLA Ops:
  0.6 16.9 %stage_one_now.1 = (bf16[1568,512]{1,0:T(8,128)(2,1)}, bf16[1568,512]{1,0:T(8,128)(2,1)}, bf16[1568,512]{1,0:T(8,128)(2,1)}, bf16[2,128,512]{2,1,0:T(8,128)(2,1)...) custom-call(bf16[6272,128]{1,0:T(8,128)(2,1)} %bitcast.10, ...), custom_call_target="tpu_custom_call" | custom-call | tf_op jit(solution)/shard_map/stage_one_now/pallas_call | solution.py:183
  17.6 26.5 %stage_two_now.1 = (bf16[1568,512]{1,0:T(8,128)(2,1)}, bf16[2,512,2048]{2,1,0:T(8,128)(2,1)}, bf16[2,2048,512]{2,1,0:T(8,128)(2,1)}, f32[2,8,1024]{2,1,0:T(8,128...) custom-call(bf16[1568,512]{1,0:T(8,128)(2,1)} %get-tuple-element.50.r_ref, ...), custom_call_target="tpu_custom_call" | custom-call | tf_op jit(solution)/shard_map/stage_two_now/pallas_call | solution.py:327
  44.1 57.8 %stage_two_back.1 = (bf16[1024,16,128]{2,1,0:T(8,128)(2,1)}, bf16[1024,16,128]{2,1,0:T(8,128)(2,1)}, bf16[128,16,128]{2,1,0:T(8,128)(2,1)}, bf16[1568,512]{1,0:T(8,128)(2,1)}) custom-call(bf16[128,512]{1,0:T(8,128)(2,1)} %get-tuple-element.51.gp_ref, bf16[1568,512]{1,0:T(8,128)(2,1)} %get-tuple-element.50.r_ref.r0_ref, ...), custom_call_target="tpu_custom_call" | custom-call | tf_op jit(solution)/shard_map/stage_two_back/pallas_call | solution.py:448
  101.9 103.0 %sum_grads.1 = (bf16[2560,16,128]{2,1,0:T(8,128)(2,1)}, f32[16,128]{1,0:T(8,128)}) custom-call(bf16[1024,16,128]{2,1,0:T(8,128)(2,1)} %get-tuple-element.57.refs_0_, bf16[1024,16,128]{2,1,0:T(8,128)(2,1)} %get-tuple-element.58.refs_1_, bf16[128,16,128]{2,1,0:T(8,128)(2,1)} %get-tuple-element.59.refs_2_, bf16[256,16,128]{2,1,0:T(8,128)(2,1)} %get-tuple-element.60.refs_3_, ...), custom_call_target="tpu_custom_call" | custom-call | tf_op jit(solution)/shard_map/sum_grads/pallas_call | solution.py:717
  204.9 18.0 %stage_one_next.1 = (bf16[1568,512]{1,0:T(8,128)(2,1)}, f32[2,128,512]{2,1,0:T(8,128)}, f32[2,512,128]{2,1,0:T(8,128)}, f32[512,512]{1,0:T(8,128)}, f32[2,128,51...) custom-call(f32[16,128]{1,0:T(8,128)} %get-tuple-element.71.sc_ref, bf16[6272,128]{1,0:T(8,128)(2,1)} %bitcast.13, ...), custom_call_target="tpu_custom_call" | custom-call | tf_op jit(solution)/shard_map/stage_one_next/pallas_call | solution.py:211
  222.9 35.0 %stage_two_next.1 = (f32[2,512,2048]{2,1,0:T(8,128)}, f32[2,2048,512]{2,1,0:T(8,128)}, f32[1000,512]{1,0:T(8,128)}, f32[2,512,2048]{2,1,0:T(8,128)}, f32[2,2048,...) custom-call(f32[16,128]{1,0:T(8,128)} %get-tuple-element.71.sc_ref, ...), custom_call_target="tpu_custom_call" | custom-call | tf_op jit(solution)/shard_map/stage_two_next/pallas_call | solution.py:377

commit v5 on v4

--- a/solution.py
+++ b/solution.py
@@ -467,7 +467,7 @@
 TOTAL = 2 * (MAIN_HALF + LATE_HALF)
 COUNTS = (512,) * 4 + (128, 256) + (32,) * 4
 SEGMENTS = (1024, 1024, 128, 256)
-LOOPS = ((0, 2), (2, 6), (6, 8))
+ENDS = (0, 1, 3, 5, 7, 8)
 HOPS = 6
 PIECES = (0, 1)
 BACKS = (0, 1, 2)
@@ -580,7 +580,7 @@
         def tell(k, turn, device):
             pl.semaphore_signal(ready.at[k, turn], device_id=(device,), device_id_type=pl.DeviceIdType.MESH)
 
-        def reduce_turn(streams, turn):
+        def reduce_turn(streams, turn, pieces=PIECES):
             if turn == HOPS - 1:
                 for k in streams:
                     for piece in PIECES:
@@ -591,10 +591,10 @@
                             copies[k, early, piece].wait_send()
                         tell(k, early, partner[plan[k][3][early]])
             if turn < 3:
-                for piece, side in enumerate((gone, kept)):
+                for piece in pieces:
                     for k in streams:
                         copies[k, turn, piece].wait_recv()
-                        dst = side[k][turn + 1]
+                        dst = (gone, kept)[piece][k][turn + 1]
                         add_in(dst, slots, slot_at(k, turn) + dst - kept[k][turn], plan[k][0], 4 >> turn)
                         if piece == 0:
                             hop(k, turn + 1)
@@ -663,29 +663,36 @@
                     grad = (ln_back(normed, inv + inv, dot_nt(grad_pre, u_ref[layer])) + grad.astype(F32)).astype(BF16)
             return carry
 
+        def after_blocks(number):
+            if number < 1:
+                first_hops(MAIN)
+            elif number < 2:
+                reduce_turn(MAIN, 0, PIECES[:1])
+            elif number < 3:
+                reduce_turn(MAIN, 0, PIECES[1:])
+                reduce_turn(MAIN, 1)
+            else:
+                reduce_turn(MAIN, number - 1)
+
         pair_up(MAIN)
-        for number, (low, high) in enumerate(LOOPS):
-            lax.fori_loop(low, high, token_block, 0)
-            if number == 0:
-                first_hops(MAIN)
-            elif number == 1:
-                reduce_turn(MAIN, 0)
+        for number in range(len(ENDS) - 1):
+            lax.fori_loop(ENDS[number], ENDS[number + 1], token_block, 0)
+            after_blocks(number)
         for layer in range(2):
             late = sum(SEGMENTS) + layer * (LATE_HALF // 2)
             put_units(flat, late, du_s[layer].astype(BF16))
             put_units(flat, late + LATE_HALF, dv_s[layer].T.astype(BF16))
         pair_up(LATE)
-        reduce_turn(MAIN, 1)
+        reduce_turn(MAIN, HOPS - 2)
         first_hops(LATE)
-        for turn in range(2, HOPS):
-            reduce_turn(MAIN, turn)
-            reduce_turn(LATE, turn - 2)
-        gather_turn(MAIN, 3)
-        reduce_turn(LATE, HOPS - 2)
-        gather_turn(MAIN, 2)
-        reduce_turn(LATE, HOPS - 1)
-        gather_turn(MAIN, 1)
-        for turn in (3, 2, 1, 0):
+        reduce_turn(MAIN, HOPS - 1)
+        reduce_turn(LATE, 0)
+        for turn in (3, 2, 1):
+            gather_turn(MAIN, turn)
+            reduce_turn(LATE, 4 - turn)
+        for turn in range(4, HOPS):
+            reduce_turn(LATE, turn)
+        for turn in reversed(range(4)):
             gather_turn(LATE, turn)
         gather_turn(MAIN, 0)
         for k in range(count):

time: 263 us -> 268 us (1.019)
  Pallas kernels: 257 us -> 262 us
    pallas_call x1, Pallas kernels: 103 us -> 108 us  [sum_grads(): pl.pallas_call(kernel, in_specs=[anywhere] * len(parts) + [vmem] * (len(s...]
where the time goes in v5:
time: 268 us; the launch traced here: 263 us
  Pallas kernels  262 us (98%)
    pallas_call x1, Pallas kernels, sum_grads(): pl.pallas_call(kernel, in_specs=[anywhere] * len(parts) + [vmem] * (len(s...  108 us
    pallas_call x1, Pallas kernels, stage_two_back(): pl.pallas_call(kernel, grid=(2, NCH), in_specs=[whole((128, W2)), act, ac...  58 us
    pallas_call x1, Pallas kernels, stage_two_next(): pl.pallas_call(kernel, grid=(2, NF), in_specs=[whole(SCALE_SHAPE), whole(...  35.1 us
    pallas_call x1, Pallas kernels, stage_two_now(): pl.pallas_call(kernel, grid=(2, NF), in_specs=[whole((ROWS, W2)), pl.Bloc...  26.2 us
    pallas_call x1, Pallas kernels, stage_one_next(): pl.pallas_call(kernel, grid=(NT,), in_specs=[whole(SCALE_SHAPE), rows_spe...  18.2 us
    pallas_call x1, Pallas kernels, stage_one_now(): pl.pallas_call(kernel, grid=(NT,), in_specs=[rows_spec(TOKENS, W1)] + [wh...  16.9 us

profile of v5, /device:TPU:1, one launch (start us, length us, event | category | flops | bytes accessed | tf_op | source)
XLA Modules:
  0.0 263.3 jit_solution(13037587223039911543)
XLA Ops:
  0.6 16.9 %stage_one_now.1 = (bf16[1568,512]{1,0:T(8,128)(2,1)}, bf16[1568,512]{1,0:T(8,128)(2,1)}, bf16[1568,512]{1,0:T(8,128)(2,1)}, bf16[2,128,512]{2,1,0:T(8,128)(2,1)...) custom-call(bf16[6272,128]{1,0:T(8,128)(2,1)} %bitcast.10, ...), custom_call_target="tpu_custom_call" | custom-call | tf_op jit(solution)/shard_map/stage_one_now/pallas_call | solution.py:183
  17.6 26.2 %stage_two_now.1 = (bf16[1568,512]{1,0:T(8,128)(2,1)}, bf16[2,512,2048]{2,1,0:T(8,128)(2,1)}, bf16[2,2048,512]{2,1,0:T(8,128)(2,1)}, f32[2,8,1024]{2,1,0:T(8,128...) custom-call(bf16[1568,512]{1,0:T(8,128)(2,1)} %get-tuple-element.50.r_ref, ...), custom_call_target="tpu_custom_call" | custom-call | tf_op jit(solution)/shard_map/stage_two_now/pallas_call | solution.py:327
  43.8 58.0 %stage_two_back.1 = (bf16[1024,16,128]{2,1,0:T(8,128)(2,1)}, bf16[1024,16,128]{2,1,0:T(8,128)(2,1)}, bf16[128,16,128]{2,1,0:T(8,128)(2,1)}, bf16[1568,512]{1,0:T(8,128)(2,1)}) custom-call(bf16[128,512]{1,0:T(8,128)(2,1)} %get-tuple-element.51.gp_ref, bf16[1568,512]{1,0:T(8,128)(2,1)} %get-tuple-element.50.r_ref.r0_ref, ...), custom_call_target="tpu_custom_call" | custom-call | tf_op jit(solution)/shard_map/stage_two_back/pallas_call | solution.py:448
  101.8 107.6 %sum_grads.1 = (bf16[2560,16,128]{2,1,0:T(8,128)(2,1)}, f32[16,128]{1,0:T(8,128)}) custom-call(bf16[1024,16,128]{2,1,0:T(8,128)(2,1)} %get-tuple-element.57.refs_0_, bf16[1024,16,128]{2,1,0:T(8,128)(2,1)} %get-tuple-element.58.refs_1_, bf16[128,16,128]{2,1,0:T(8,128)(2,1)} %get-tuple-element.59.refs_2_, bf16[256,16,128]{2,1,0:T(8,128)(2,1)} %get-tuple-element.60.refs_3_, ...), custom_call_target="tpu_custom_call" | custom-call | tf_op jit(solution)/shard_map/sum_grads/pallas_call | solution.py:724
  209.4 18.2 %stage_one_next.1 = (bf16[1568,512]{1,0:T(8,128)(2,1)}, f32[2,128,512]{2,1,0:T(8,128)}, f32[2,512,128]{2,1,0:T(8,128)}, f32[512,512]{1,0:T(8,128)}, f32[2,128,51...) custom-call(f32[16,128]{1,0:T(8,128)} %get-tuple-element.71.sc_ref, bf16[6272,128]{1,0:T(8,128)(2,1)} %bitcast.13, ...), custom_call_target="tpu_custom_call" | custom-call | tf_op jit(solution)/shard_map/stage_one_next/pallas_call | solution.py:211
  227.6 35.1 %stage_two_next.1 = (f32[2,512,2048]{2,1,0:T(8,128)}, f32[2,2048,512]{2,1,0:T(8,128)}, f32[1000,512]{1,0:T(8,128)}, f32[2,512,2048]{2,1,0:T(8,128)}, f32[2,2048,...) custom-call(f32[16,128]{1,0:T(8,128)} %get-tuple-element.71.sc_ref, ...), custom_call_target="tpu_custom_call" | custom-call | tf_op jit(solution)/shard_map/stage_two_next/pallas_call | solution.py:377
